TPU v7x, 32 devices: a whole 2x2x4 slice. The times are simulated.
32 devices in a mesh: hist: 8 (over y, x, core), col: 4 (over z).
Axes of the slice: x: 2, y: 2, z: 4, core: 2. Of those that a mesh axis runs over, the one named last changes fastest.
Arguments:
- less_row: bfloat16 [2, 128, 128, 1024], P(None, None, 'col', 'hist'), may hold values from -1.796875 to 1.796875
- less_col: bfloat16 [2, 128, 128, 1024], P(None, None, 'col', 'hist'), may hold values from -1.796875 to 1.796875
- great_row: bfloat16 [2, 128, 128, 1024], P(None, None, 'col', 'hist'), may hold values from -1.796875 to 1.796875
- great_col: bfloat16 [2, 128, 128, 1024], P(None, None, 'col', 'hist'), may hold values from -1.796875 to 1.796875
- density: float32 [2, 128, 128], replicated, may hold values from -1.8 to 1.8
- hamiltonian: float32 [128, 128], replicated, may hold values from -0.5 to 0.5
Outputs:
- less_row_out: bfloat16 [2, 128, 128, 1024], P(None, None, 'col', 'hist')
- less_col_out: bfloat16 [2, 128, 128, 1024], P(None, None, 'col', 'hist')
- great_row_out: bfloat16 [2, 128, 128, 1024], P(None, None, 'col', 'hist')
- great_col_out: bfloat16 [2, 128, 128, 1024], P(None, None, 'col', 'hist')
- density_out: float32 [2, 128, 128], replicated
All inputs are finite; a program needn't handle non-finite values.
Results may differ from a plain program's by a relative error of at most 0.033.
Values may be sent and summed in bfloat16 or wider, within the bound.
No kernel may reach another device: no remote copies, remote signals or barrier semaphores. Data moves between devices by JAX's collectives and lax.ppermute only.
A program may use at most 128 MiB of HBM per device.

v0:
```python
import functools

import jax
import jax.numpy as jnp
from jax import lax
from jax.experimental import pallas as pl
from jax.experimental.pallas import tpu as pltpu
from jax.sharding import PartitionSpec as P


step_length = 0.1
mean_field = 2.0
coupling = 1.0

HIGH = lax.Precision.HIGHEST
SUBLANES = 8
GROUP = 8
SPAN = 256


def dot_high(a, b):
    return jnp.dot(a, b, precision=HIGH, preferred_element_type=jnp.float32)


def eye_mask(size):
    rows = lax.broadcasted_iota(jnp.int32, (size, size), 0)
    return rows == lax.broadcasted_iota(jnp.int32, (size, size), 1)


def inverse(matrix):
    size = matrix.shape[0]
    blocks = [matrix[p : p + SUBLANES] for p in range(0, size, SUBLANES)]
    rows = lax.broadcasted_iota(jnp.int32, (SUBLANES, size), 0)
    lanes = lax.broadcasted_iota(jnp.int32, (SUBLANES, size), 1)
    for p in range(len(blocks)):
        first = p * SUBLANES
        pivot_lanes = (lanes >= first) & (lanes < first + SUBLANES)

        def columns(block):
            return [jnp.broadcast_to(block[:, first + c : first + c + 1], (SUBLANES, size)) for c in range(SUBLANES)]

        pivot = columns(blocks[p])
        row_block = jnp.where(pivot_lanes, jnp.where(lanes == rows + first, 1.0, 0.0), blocks[p])
        for j in range(SUBLANES):

            def across(value):
                return jnp.broadcast_to(value[j : j + 1], (SUBLANES, size))

            scale = 1.0 / across(pivot[j])
            factor = pivot[j]

            def eliminate(value):
                top = across(value) * scale
                return jnp.where(rows == j, top, value - factor * top)

            row_block = eliminate(row_block)
            pivot = [eliminate(value) if c > j else value for c, value in enumerate(pivot)]
        spread = [jnp.broadcast_to(row_block[c : c + 1], (SUBLANES, size)) for c in range(SUBLANES)]
        order = list(range(p + 1, len(blocks))) + list(range(p))
        for q in order:
            total = jnp.where(pivot_lanes, 0.0, blocks[q])
            for c, column in enumerate(columns(blocks[q])):
                total = total - column * spread[c]
            blocks[q] = total
        blocks[p] = row_block
    return jnp.concatenate(blocks, axis=0)


def spread_rows(ref, row):
    ref[...] = jnp.broadcast_to(row.reshape(1, 1, row.shape[-1]), ref.shape)


def diagonal_row(matrix):
    return jnp.sum(jnp.where(eye_mask(matrix.shape[0]), matrix, 0.0), axis=0, keepdims=True)


def solve_kernel(rotates, levels_ref, ham_ref, *refs):
    size = ham_ref.shape[0]
    eye = eye_mask(size)
    level = levels_ref[0]
    for row in range(1, levels_ref.shape[0]):
        level = level + levels_ref[row]
    halved = (0.5 * step_length) * (ham_ref[...] + mean_field * jnp.where(eye, level, 0.0))
    identity = jnp.where(eye, 1.0, 0.0)
    solved = inverse(identity + dot_high(halved, halved))
    unit_real = 2.0 * solved - identity
    unit_imag = -2.0 * dot_high(solved, halved)
    low_real, low_imag = unit_real.astype(jnp.bfloat16), unit_imag.astype(jnp.bfloat16)
    if rotates:
        rho_ref, later_ref, low_ref, unit_ref, left_ref, next_ref = refs
    else:
        low_ref, unit_ref = refs
    low_ref[0:size, 0:size] = low_real
    low_ref[0:size, size:] = low_imag
    low_ref[size:, 0:size] = -low_imag
    low_ref[size:, size:] = low_real
    unit_ref[0] = unit_real
    unit_ref[1] = unit_imag
    if rotates:
        rho_real, rho_imag = rho_ref[0], rho_ref[1]
        left_real = dot_high(unit_real, rho_real) - dot_high(unit_imag, rho_imag)
        left_imag = dot_high(unit_real, rho_imag) + dot_high(unit_imag, rho_real)
        left_ref[0] = left_real
        left_ref[1] = left_imag
        real_diagonal = jnp.sum(left_real * unit_real + left_imag * unit_imag, axis=1, keepdims=True)
        row = jnp.sum(jnp.where(eye, real_diagonal + later_ref[0], 0.0), axis=0, keepdims=True)
        spread_rows(next_ref, row)


IN_VMEM = pl.BlockSpec(memory_space=pltpu.VMEM)
GRANT = pltpu.CompilerParams(vmem_limit_bytes=8 * 2**20)


def call(body, outs, args, cost_estimate, scratch=(), scalars=0):
    specs = [pl.BlockSpec(memory_space=pltpu.SMEM)] * scalars + [IN_VMEM] * (len(args) - scalars)
    return pl.pallas_call(
        body,
        out_shape=[jax.ShapeDtypeStruct(shape, kind) for shape, kind in outs],
        in_specs=specs,
        out_specs=[IN_VMEM] * len(outs),
        scratch_shapes=list(scratch),
        cost_estimate=cost_estimate,
        compiler_params=GRANT,
    )(*args)


def solve(levels, hamiltonian, rho=None, later=None):
    size = hamiltonian.shape[0]
    outs = [((2 * size, 2 * size), jnp.bfloat16), ((2, size, size), jnp.float32)]
    args = (levels, hamiltonian)
    if rho is not None:
        outs += [((2, size, size), jnp.float32), (levels.shape, jnp.float32)]
        args += (rho, later)
    estimate = pl.CostEstimate(flops=4_000_000_000, bytes_accessed=1_000_000, transcendentals=0)
    return call(functools.partial(solve_kernel, rho is not None), outs, args, estimate)


def lanes_of(base, first, span):
    return pl.ds(pl.multiple_of(base + first, 128), span)


def sigma_into(sig_ref, row_ref, col_ref, base, rows, span):
    size = sig_ref.shape[0] // 2
    for start in range(0, size, rows):
        for first in range(0, sig_ref.shape[1], span):
            real, imag = pl.ds(start, rows), pl.ds(size + start, rows)
            lanes, here = lanes_of(base, first, span), pl.ds(first, span)
            green_real = row_ref[real, lanes].astype(jnp.float32)
            green_imag = row_ref[imag, lanes].astype(jnp.float32)
            other_real = col_ref[real, lanes].astype(jnp.float32)
            other_imag = col_ref[imag, lanes].astype(jnp.float32)
            square_real = (coupling * coupling) * (green_real * green_real - green_imag * green_imag)
            square_imag = (coupling * coupling * 2.0) * green_real * green_imag
            sig_ref[real, here] = (square_real * other_real - square_imag * other_imag).astype(jnp.bfloat16)
            sig_ref[imag, here] = (square_real * other_imag + square_imag * other_real).astype(jnp.bfloat16)


def overlap(sig, col):
    return lax.dot_general(sig, col, (((1,), (1,)), ((), ())), preferred_element_type=jnp.float32)


def advance_into(out_ref, low, source_ref, base, width, local=False):
    span = min(SPAN, width)
    for first in range(0, width, span):
        lanes = lanes_of(base, first, span)
        target = pl.ds(first, span) if local else lanes
        moved = jnp.dot(low, source_ref[:, lanes], preferred_element_type=jnp.float32)
        out_ref[:, target] = moved.astype(out_ref.dtype)


def row_form(low):
    size = low.shape[0] // 2
    top = jnp.concatenate([low[:size, :size], low[size:, :size]], axis=1)
    bottom = jnp.concatenate([low[:size, size:], low[:size, :size]], axis=1)
    return jnp.concatenate([top, bottom], axis=0)


def each_group(total_width, width, body):
    def step(g, carry):
        body(pl.multiple_of(g * width, width))
        return carry

    lax.fori_loop(0, total_width // width, step, 0)


def complex_sum(four):
    size = four.shape[0] // 2
    return four[:size, :size] - four[size:, size:], four[:size, size:] + four[size:, :size]


def finish_sum(acc, before_ref, base_ref, out_ref, scale):
    real, imag = complex_sum(scale * (acc[...] - before_ref[...]))
    if base_ref is not None:
        real, imag = base_ref[0] + real, base_ref[1] + imag
    out_ref[0] = real
    out_ref[1] = imag
    return real


def now_kernel(parts, last, me_ref, row_ref, own_ref, *refs):
    pieces, refs = refs[: parts - 1], refs[parts - 1 :]
    if last:
        before_ref, known_ref, col_out, rho_out, level_out, acc, sig, place = refs
    else:
        col_out, acc, sig, place = refs
    _, count, block, times = pieces[0].shape
    width = sig.shape[1]
    group = width // times
    size = sig.shape[0] // 2
    direct = place.dtype == col_out.dtype
    acc[...] = jnp.zeros_like(acc)

    def body(base):
        first = lax.div(base, times)
        for r in range(parts):
            source = lax.bitwise_xor(me_ref[0], r) * block
            for part in range(2):
                rows = pl.ds(pl.multiple_of(part * size + source, block), block)
                for k in range(group):
                    if r == 0:
                        value = own_ref[part, me_ref[0] * count + first + k]
                    else:
                        value = pieces[r - 1][part, first + k]
                    if direct:
                        col_out[rows, lanes_of(base, k * times, times)] = value
                    else:
                        place[rows, pl.ds(k * times, times)] = value.astype(place.dtype)
        if not direct:
            col_out[:, lanes_of(base, 0, width)] = place[...].astype(col_out.dtype)
        sigma_into(sig, row_ref, col_out, base, 16, min(SPAN, width))
        acc[...] += overlap(sig[...], col_out[:, lanes_of(base, 0, width)])

    each_group(col_out.shape[1], width, body)
    if last:
        real = finish_sum(acc, before_ref, known_ref, rho_out, step_length)
        spread_rows(level_out, diagonal_row(real))


def later_kernel(last, row_ref, col_ref, low_ref, *refs):
    if last:
        before_ref, row_out, col_out, sum_out, acc, sig = refs
    else:
        row_out, col_out, acc, sig = refs
    width = sig.shape[1]
    acc[...] = jnp.zeros_like(acc)

    def body(base):
        advance_into(row_out, row_form(low_ref[...]), row_ref, base, width)
        advance_into(col_out, low_ref[...], col_ref, base, width)
        sigma_into(sig, row_out, col_out, base, 16, min(SPAN, width))
        acc[...] += overlap(sig[...], col_out[:, lanes_of(base, 0, width)])

    each_group(col_out.shape[1], width, body)
    if last:
        finish_sum(acc, before_ref, None, sum_out, step_length)


def finish_kernel(left_ref, unit_ref, later_ref, unit_last_ref, last_ref, rho_ref):
    def right(real, imag, unit):
        turned_real, turned_imag = unit[0].T, unit[1].T
        return (
            dot_high(real, turned_real) + dot_high(imag, turned_imag),
            dot_high(imag, turned_real) - dot_high(real, turned_imag),
        )

    real, imag = right(left_ref[0], left_ref[1], unit_ref)
    real, imag = real + later_ref[0], imag + later_ref[1]
    unit_real, unit_imag = unit_last_ref[0], unit_last_ref[1]
    left_real = dot_high(unit_real, real) - dot_high(unit_imag, imag)
    left_imag = dot_high(unit_real, imag) + dot_high(unit_imag, real)
    real, imag = right(left_real, left_imag, unit_last_ref)
    rho_ref[0] = real + last_ref[0]
    rho_ref[1] = imag + last_ref[1]


def row_kernel(width, row_ref, low_ref, row_out):
    low = row_form(low_ref[...])
    each_group(row_ref.shape[1], width, lambda base: advance_into(row_out, low, row_ref, base, width))


def last_kernel(parts, me_ref, col_ref, low_ref, *refs):
    outs, moved = refs[:parts], refs[parts]
    _, _, block, times = outs[0].shape
    width = moved.shape[1]
    size = moved.shape[0] // 2
    low = low_ref[...]

    def body(base):
        first = lax.div(base, times)
        advance_into(moved, low, col_ref, base, width, local=True)
        for r in range(parts):
            target = lax.bitwise_xor(me_ref[0], r) * block
            for part in range(2):
                rows = pl.ds(pl.multiple_of(part * size + target, block), block)
                for k in range(width // times):
                    outs[r][part, first + k] = moved[rows, pl.ds(k * times, times)].astype(outs[r].dtype)

    each_group(col_ref.shape[1], width, body)


def cost(arrays, products):
    return pl.CostEstimate(flops=products * 2 * 256 * 256 * 4096, bytes_accessed=arrays * 2**21, transcendentals=0)


def place_type(block):
    return jnp.bfloat16 if block % 16 == 0 else jnp.float32


def sum_scratch(size, width):
    return [pltpu.VMEM((2 * size, 2 * size), jnp.float32), pltpu.VMEM((2 * size, width), jnp.bfloat16)]


def now_step(me, row, own, pieces, before=None, known=None, devices=0):
    size = own.shape[1]
    _, count, block, times = pieces[0].shape
    width = min(GROUP, count) * times
    square, history = ((2 * size, 2 * size), jnp.float32), (row.shape, jnp.bfloat16)
    args = (me, row, own, *pieces)
    place = pltpu.VMEM((2 * size, width), place_type(block))
    sig = pltpu.VMEM((2 * size, width), jnp.bfloat16)
    body = functools.partial(now_kernel, len(pieces) + 1, before is not None)
    if before is None:
        return call(body, [history, square], args, cost(4, 2), [sig, place], 1)
    outs = [history, ((2, size, size), jnp.float32), ((devices, 1, size), jnp.float32)]
    scratch = sum_scratch(size, width) + [place]
    return call(body, outs, args + (before, known), cost(4, 2), scratch, 1)


def later_step(row, col, low, width, before=None):
    double = row.shape[0]
    square, history = ((double, double), jnp.float32), (row.shape, jnp.bfloat16)
    body = functools.partial(later_kernel, before is not None)
    if before is None:
        scratch = [pltpu.VMEM((double, width), jnp.bfloat16)]
        return call(body, [history, history, square], (row, col, low), cost(4, 3), scratch)
    outs = [history, history, ((2, double // 2, double // 2), jnp.float32)]
    return call(body, outs, (row, col, low, before), cost(4, 3), sum_scratch(double // 2, width))


def row_step(row, low, width):
    body = functools.partial(row_kernel, width)
    return call(body, [(row.shape, jnp.bfloat16)], (row, low), cost(2, 1))[0]


def last_step(me, col, low, parts, count, times):
    double = col.shape[0]
    block = double // 2 // parts
    width = min(GROUP, count) * times
    outs = [((2, count, block, times), jnp.bfloat16)] * parts
    scratch = [pltpu.VMEM((double, width), place_type(block))]
    body = functools.partial(last_kernel, parts)
    return call(body, outs, (me, col, low), cost(2, 1), scratch, 1)


def tree_sum(values):
    while len(values) > 1:
        values = [values[i] + values[i + 1] for i in range(0, len(values), 2)]
    return values[0]


def swap(value, name, r):
    return lax.ppermute(value, name, [(j, j ^ r) for j in range(lax.axis_size(name))])


def part_total(values):
    count = lax.axis_size("hist")
    rows = values.reshape(count, -1, values.shape[-1])
    share = jnp.sum(lax.all_to_all(rows, "hist", 0, 0, tiled=True), axis=0)
    return share


def whole_total(share, shape):
    count = lax.axis_size("hist")
    moved = [share] + [swap(share, "col", r) for r in range(1, lax.axis_size("col"))]
    share = tree_sum(moved)
    return lax.all_to_all(jnp.broadcast_to(share, (count,) + share.shape), "hist", 0, 0, tiled=True).reshape(shape)


def finish_rotation(left, unit):
    high = functools.partial(jnp.dot, precision=HIGH)
    real = high(left[0], unit[0].T) + high(left[1], unit[1].T)
    imag = high(left[1], unit[0].T) - high(left[0], unit[1].T)
    return jnp.stack([real, imag])


def rotate(unit, rho):
    high = functools.partial(jnp.dot, precision=HIGH)
    real = high(unit[0], rho[0]) - high(unit[1], rho[1])
    imag = high(unit[0], rho[1]) + high(unit[1], rho[0])
    return finish_rotation((real, imag), unit)


def gather_pieces(col):
    me, parts = lax.axis_index("col"), lax.axis_size("col")
    count = col.shape[1] // parts
    pieces = []
    for r in range(1, parts):
        piece = lax.dynamic_slice_in_dim(col, (me ^ r) * count, count, axis=1)
        pieces.append(swap(piece, "col", r))
    return pieces


def return_pieces(pieces):
    me, parts = lax.axis_index("col"), lax.axis_size("col")
    _, count, block, times = pieces[0].shape
    out = jnp.zeros((2, parts * count, block, times), pieces[0].dtype)
    for r, piece in enumerate(pieces):
        moved = piece if r == 0 else swap(piece, "col", r)
        out = lax.dynamic_update_slice_in_dim(out, moved, (me ^ r) * count, axis=1)
    return out


def per_device(less_row, less_col, great_row, great_col, density, hamiltonian):
    size, count, times = less_row.shape[1:]
    parts = lax.axis_size("col")
    devices = parts * lax.axis_size("hist")
    me = lax.axis_index("col").astype(jnp.int32).reshape(1)
    width = min(GROUP, count) * times

    great_pieces = gather_pieces(great_col)
    less_pieces = gather_pieces(less_col)

    symmetric = 0.5 * (hamiltonian + hamiltonian.T)
    low, unit = solve(diagonal_row(density[0]).reshape(1, 1, size), symmetric)
    known = rotate(unit, density * (1.0 / devices))

    less = less_row.reshape(2 * size, count * times)
    great = great_row.reshape(2 * size, count * times)
    cols_great, minus = now_step(me, less, great_col, great_pieces)
    less, cols_great, minus_later = later_step(less, cols_great, low, width)
    less_pieces, minus_later = lax.optimization_barrier((less_pieces, minus_later))
    cols_less, rho, part = now_step(me, great, less_col, less_pieces, minus, known, devices)

    levels = lax.all_to_all(part, ("hist", "col"), 0, 0, tiled=True)
    great, cols_less, later = later_step(great, cols_less, low, width, minus_later)
    low, unit, left, part = solve(levels, symmetric, rho, later)

    levels = lax.all_to_all(part, ("hist", "col"), 0, 0, tiled=True)
    less, cols_great, minus = later_step(less, cols_great, low, width)
    great, cols_less, last = later_step(great, cols_less, low, width, minus)
    low, unit_last = solve(levels, symmetric)

    great_out = return_pieces(last_step(me, cols_great, low, parts, count, times))
    args = (left, unit, later, unit_last, last)
    estimate = pl.CostEstimate(flops=500_000_000, bytes_accessed=1_000_000, transcendentals=0)
    rho = call(finish_kernel, [(density.shape, jnp.float32)], args, estimate)[0]
    share = part_total(rho)
    cols_less, share = lax.optimization_barrier((cols_less, share))
    less_out = return_pieces(last_step(me, cols_less, low, parts, count, times))
    rho = whole_total(share, density.shape)
    less_row_out = row_step(less, low, width).reshape(less_row.shape)
    great_row_out = row_step(great, low, width).reshape(great_row.shape)
    return (less_row_out, less_out, great_row_out, great_out, rho)


def solution(mesh):
    history = P(None, None, "col", "hist")
    return jax.shard_map(
        per_device,
        mesh=mesh,
        in_specs=(history, history, history, history, P(), P()),
        out_specs=(history, history, history, history, P()),
        check_vma=False,
    )
```

profile of v0, /device:TPU:10, one launch (start us, length us, event | category | flops | bytes accessed | tf_op | source)
XLA Modules:
  0.0 255.8 jit_solution(4080017098512622940)
XLA Ops:
  0.7 2.7 %constant_dynamic-slice_fusion.3 = (bf16[2,32,32,128]{3,2,1,0:T(8,128)(2,1)}, bf16[2,32,32,128]{3,2,1,0:T(8,128)(2,1)}, bf16[2,32,32,128]{3,2,1,0:T(8,128)(2,1)}) fusion(bf16[2,128,32,128]{3,2,1,0:T(8,128)(2,1)} %own_ref.2, s32[]{:T(128)S(6)} %select_n.14, s32[]{:T(128)S(6)} %select_n.13, s32[]{:T(128)S(6)} %select_n.12), kind=kLoop, calls=%fused_computation.49 | loop fusion | bytes 3145740 | tf_op jit(solution)/shard_map/dynamic_slice | solution.py:398
  3.8 2.6 %collective-permute-start.1 = (bf16[2,32,32,128]{3,2,1,0:T(8,128)(2,1)}, bf16[2,32,32,128]{3,2,1,0:T(8,128)(2,1)}, u32[]{:S(2)}, u32[]{:S(2)}) collective-permute-start(bf16[2,32,32,128]{3,2,1,0:T(8,128)(2,1)} %get-tuple-element.87), channel_id=1, source_target_pairs={{0,2},{1,3},{2,0},{3,1},{4,6},{5,7},{6,4},{7,5},{8,10},{9,11},{10,... | collective-permute-start | bytes 1572872 | tf_op jit(solution)/shard_map/ppermute | solution.py:362
  8.0 1.3 collective-permute-start.3
  9.4 2.1 collective-permute-start.4
  11.7 4.4 %shard_map.102 = (bf16[256,256]{1,0:T(8,128)(2,1)S(1)}, f32[2,128,128]{2,1,0:T(8,128)S(1)}) custom-call(f32[1,1,128]{2,1,0:T(1,128)S(1)} %bitcast.68, f32[128,128]{1,0:T(8,128)S(1)} %fusion.14.ham_ref), custom_call_target="tpu_custom_call" | custom-call | flops 4000000000 | bytes 1000000 | tf_op jit(solution)/shard_map/pallas_call | solution.py:116
  18.1 8.8 %collective-permute-done.refs_0_ = bf16[2,32,32,128]{3,2,1,0:T(8,128)(2,1)} collective-permute-done((bf16[2,32,32,128]{3,2,1,0:T(8,128)(2,1)}, bf16[2,32,32,128]{3,2,1,0:T(8,128)(2,1)}, u32[]{:S(2)}, u32[]{:S(2)}) %collective-permute-start) | collective-permute-done | bytes 524320 | tf_op jit(solution)/shard_map/ppermute | solution.py:362
  26.9 2.7 %collective-permute-start.5 = (bf16[2,32,32,128]{3,2,1,0:T(8,128)(2,1)}, bf16[2,32,32,128]{3,2,1,0:T(8,128)(2,1)}, u32[]{:S(2)}, u32[]{:S(2)}) collective-permute-start(bf16[2,32,32,128]{3,2,1,0:T(8,128)(2,1)} %get-tuple-element.83), channel_id=1, source_target_pairs={{0,3},{1,2},{2,1},{3,0},{4,7},{5,6},{6,5},{7,4},{8,11},{9,10},{10,... | collective-permute-start | bytes 1572872 | tf_op jit(solution)/shard_map/ppermute | solution.py:362
  30.5 4.0 %copy.19 = bf16[32,8,32,128]{3,1,2,0:T(8,128)(2,1)} copy(bf16[32,8,32,128]{3,2,1,0:T(8,128)(2,1)} %bitcast.69) | data formatting | bytes 4194304
  37.5 4.0 %collective-permute-done.1.refs_1_ = bf16[2,32,32,128]{3,2,1,0:T(8,128)(2,1)} collective-permute-done((bf16[2,32,32,128]{3,2,1,0:T(8,128)(2,1)}, bf16[2,32,32,128]{3,2,1,0:T(8,128)(2,1)}, u32[]{:S(2)}, u32[]{:S(2)}) %collective-permute-start.1) | collective-permute-done | bytes 524320 | tf_op jit(solution)/shard_map/ppermute | solution.py:362
  41.5 34.6 %collective-permute-done.2.refs_2_ = bf16[2,32,32,128]{3,2,1,0:T(8,128)(2,1)} collective-permute-done((bf16[2,32,32,128]{3,2,1,0:T(8,128)(2,1)}, bf16[2,32,32,128]{3,2,1,0:T(8,128)(2,1)}, u32[]{:S(2)}, u32[]{:S(2)}) %collective-permute-start.2) | collective-permute-done | bytes 524320 | tf_op jit(solution)/shard_map/ppermute | solution.py:362
  76.1 1.6 copy-done
  77.7 1.6 copy-done.2
  79.3 3.8 %shard_map.101 = (bf16[256,4096]{1,0:T(8,128)(2,1)S(1)}, f32[256,256]{1,0:T(8,128)S(1)}) custom-call(s32[1]{0:T(128)} %bitcast.me_ref, bf16[256,4096]{1,0:T(8,128)(2,1)S(1)} %bitcast.64, bf16[2,128,32,128]{3,2,1,0:T(8,128)(2,1)S(1)} %copy-done.2, bf16[2,32,32,128]{3,2,1,0:T(8,128)(2,1)} %collective-permute-done.refs_0_, ...), custom_call_target="tpu_custom_call" | custom-call | flops 1073741824 | bytes 8388608 | tf_op jit(solution)/shard_map/pallas_call | solution.py:116
  83.2 4.4 %shard_map.103 = (bf16[256,4096]{1,0:T(8,128)(2,1)S(1)}, bf16[256,4096]{1,0:T(8,128)(2,1)S(1)}, f32[256,256]{1,0:T(8,128)S(1)}) custom-call(bf16[256,4096]{1,0:T(8,128)(2,1)S(1)} %bitcast.65, bf16[256,4096]{1,0:T(8,128)(2,1)S(1)} %get-tuple-element.44.col_ref, bf16[256,256]{1,0:T(8,128)(2,1)S(1)} %get-tuple-element.45.low_ref), custom_call_target="tpu_custom_call" | custom-call | flops 1610612736 | bytes 8388608 | tf_op jit(solution)/shard_map/pallas_call | solution.py:116
  90.2 7.0 %collective-permute-done.5.refs_2_ = bf16[2,32,32,128]{3,2,1,0:T(8,128)(2,1)} collective-permute-done((bf16[2,32,32,128]{3,2,1,0:T(8,128)(2,1)}, bf16[2,32,32,128]{3,2,1,0:T(8,128)(2,1)}, u32[]{:S(2)}, u32[]{:S(2)}) %collective-permute-start.5) | collective-permute-done | bytes 524320 | tf_op jit(solution)/shard_map/ppermute | solution.py:362
  97.3 4.1 %shard_map.104 = (bf16[256,4096]{1,0:T(8,128)(2,1)S(1)}, f32[2,128,128]{2,1,0:T(8,128)S(1)}, f32[32,1,128]{2,1,0:T(1,128)}) custom-call(s32[1]{0:T(128)} %bitcast.me_ref, bf16[256,4096]{1,0:T(8,128)(2,1)S(1)} %bitcast.62, bf16[2,128,32,128]{3,2,1,0:T(8,128)(2,1)S(1)} %copy-done.4, bf16[2,32,32,128]{3,2,1,0:T(8,128)(2,1)S(1)} %collective-permute-done.3.refs_0_, ...), custom_call_target="tpu_custom_call" | custom-call | flops 1073741824 | bytes 8388608 | tf_op jit(solution)/shard_map/pallas_call | solution.py:116
  102.6 5.0 %all-to-all-start = ((f32[32,1,128]{2,1,0:T(1,128)}), f32[32,1,128]{2,1,0:T(1,128)S(1)}, u32[]{:S(2)}, u32[]{:S(2)}) async-start(f32[32,1,128]{2,1,0:T(1,128)} %get-tuple-element.54), calls=%async_computation | async-start | bytes 32768 | tf_op jit(solution)/shard_map/all_to_all | solution.py:434
  107.7 1.6 copy-done.12
  111.1 4.4 %shard_map.105 = (bf16[256,4096]{1,0:T(8,128)(2,1)S(1)}, bf16[256,4096]{1,0:T(8,128)(2,1)S(1)}, f32[2,128,128]{2,1,0:T(8,128)S(1)}) custom-call(bf16[256,4096]{1,0:T(8,128)(2,1)S(1)} %bitcast.63, bf16[256,4096]{1,0:T(8,128)(2,1)S(1)} %copy-done.12, bf16[256,256]{1,0:T(8,128)(2,1)S(1)} %copy-done.26, f32[256,256]{1,0:T(8,128)S(1)} %copy-done.24), custom_call_target="tpu_custom_call" | custom-call | flops 1610612736 | bytes 8388608 | tf_op jit(solution)/shard_map/pallas_call | solution.py:116
  118.1 5.4 %shard_map.106 = (bf16[256,256]{1,0:T(8,128)(2,1)S(1)}, f32[2,128,128]{2,1,0:T(8,128)S(1)}, f32[2,128,128]{2,1,0:T(8,128)S(1)}, f32[32,1,128]{2,1,0:T(1,128)}) custom-call(f32[32,1,128]{2,1,0:T(1,128)S(1)} %all-to-all-done.levels_ref, f32[128,128]{1,0:T(8,128)S(1)} %fusion.14.ham_ref, f32[2,128,128]{2,1,0:T(8,128)S(1)} %get-tuple-element.55.refs_0_, ...), custom_call_target="tpu_custom_call" | custom-call | flops 4000000000 | bytes 1000000 | tf_op jit(solution)/shard_map/pallas_call | solution.py:116
  123.6 5.8 %all-to-all-start.1 = ((f32[32,1,128]{2,1,0:T(1,128)}), f32[32,1,128]{2,1,0:T(1,128)S(1)}, u32[]{:S(2)}, u32[]{:S(2)}) async-start(f32[32,1,128]{2,1,0:T(1,128)} %get-tuple-element.61), calls=%async_computation.1 | async-start | bytes 32768 | tf_op jit(solution)/shard_map/all_to_all | solution.py:438
  129.4 1.6 copy-done.22
  131.0 4.4 %shard_map.107 = (bf16[256,4096]{1,0:T(8,128)(2,1)S(1)}, bf16[256,4096]{1,0:T(8,128)(2,1)S(1)}, f32[256,256]{1,0:T(8,128)S(1)}) custom-call(bf16[256,4096]{1,0:T(8,128)(2,1)S(1)} %copy-done.20, bf16[256,4096]{1,0:T(8,128)(2,1)S(1)} %copy-done.22, bf16[256,256]{1,0:T(8,128)(2,1)S(1)} %get-tuple-element.59.low_ref), custom_call_target="tpu_custom_call" | custom-call | flops 1610612736 | bytes 8388608 | tf_op jit(solution)/shard_map/pallas_call | solution.py:116
  135.4 1.3 copy-done.5
  138.1 4.4 %shard_map.110 = (bf16[256,4096]{1,0:T(8,128)(2,1)S(1)}, bf16[256,4096]{1,0:T(8,128)(2,1)S(1)}, f32[2,128,128]{2,1,0:T(8,128)S(1)}) custom-call(bf16[256,4096]{1,0:T(8,128)(2,1)S(1)} %copy-done.16, bf16[256,4096]{1,0:T(8,128)(2,1)S(1)} %copy-done.18, bf16[256,256]{1,0:T(8,128)(2,1)S(1)} %get-tuple-element.59.low_ref, f32[256,256]{1,0:T(8,128)S(1)} %get-tuple-element.65.refs_0_), custom_call_target="tpu_custom_call" | custom-call | flops 1610612736 | bytes 8388608 | tf_op jit(solution)/shard_map/pallas_call | solution.py:116
  143.8 4.4 %shard_map.108 = (bf16[256,256]{1,0:T(8,128)(2,1)S(1)}, f32[2,128,128]{2,1,0:T(8,128)S(1)}) custom-call(f32[32,1,128]{2,1,0:T(1,128)S(1)} %all-to-all-done.1.levels_ref, f32[128,128]{1,0:T(8,128)S(1)} %fusion.14.ham_ref), custom_call_target="tpu_custom_call" | custom-call | flops 4000000000 | bytes 1000000 | tf_op jit(solution)/shard_map/pallas_call | solution.py:116
  148.2 2.2 shard_map.111
  150.5 4.2 %all-to-all-start.2 = ((f32[8,32,128]{2,1,0:T(8,128)}), f32[8,32,128]{2,1,0:T(8,128)S(1)}, u32[]{:S(2)}, u32[]{:S(2)}) async-start(f32[8,32,128]{2,1,0:T(8,128)} %bitcast.10), calls=%async_computation.2 | async-start | bytes 262144 | tf_op jit(solution)/shard_map/all_to_all | solution.py:368
  154.7 1.6 copy-done.6
  156.3 2.6 %shard_map.114 = (bf16[2,32,32,128]{3,2,1,0:T(8,128)(2,1)S(1)}, bf16[2,32,32,128]{3,2,1,0:T(8,128)(2,1)}, bf16[2,32,32,128]{3,2,1,0:T(8,128)(2,1)}, bf16[2,32,32,128]{3,2,1,0:T(8,128)(2,1)S(1)}) custom-call(s32[1]{0:T(128)} %bitcast.me_ref, bf16[256,4096]{1,0:T(8,128)(2,1)S(1)} %copy-done.6, bf16[256,256]{1,0:T(8,128)(2,1)S(1)} %get-tuple-element.62.low_ref), custom_call_target="tpu_custom_call" | custom-call | flops 536870912 | bytes 4194304 | tf_op jit(solution)/shard_map/pallas_call | solution.py:116
  159.4 2.4 collective-permute-start.10
  163.1 1.8 copy.15
  166.3 1.8 copy.14
  168.1 1.6 broadcast.3.clone.1
  170.6 1.6 collective-permute-start.12
  172.7 1.5 collective-permute-start.14
  174.2 2.6 %shard_map.112 = (bf16[2,32,32,128]{3,2,1,0:T(8,128)(2,1)S(1)}, bf16[2,32,32,128]{3,2,1,0:T(8,128)(2,1)}, bf16[2,32,32,128]{3,2,1,0:T(8,128)(2,1)}, bf16[2,32,32,128]{3,2,1,0:T(8,128)(2,1)S(1)}) custom-call(s32[1]{0:T(128)} %bitcast.me_ref, bf16[256,4096]{1,0:T(8,128)(2,1)S(1)} %get-tuple-element.71.col_ref, bf16[256,256]{1,0:T(8,128)(2,1)S(1)} %get-tuple-element.62.low_ref), custom_call_target="tpu_custom_call" | custom-call | flops 536870912 | bytes 4194304 | tf_op jit(solution)/shard_map/pallas_call | solution.py:116
  177.5 7.4 %collective-permute-done.12 = f32[32,128]{1,0:T(8,128)S(1)} collective-permute-done((f32[32,128]{1,0:T(8,128)S(1)}, f32[32,128]{1,0:T(8,128)S(1)}, u32[]{:S(2)}, u32[]{:S(2)}) %collective-permute-start.12) | collective-permute-done | bytes 16416 | tf_op jit(solution)/shard_map/ppermute | solution.py:362
  185.0 1.5 collective-permute-start.11
  186.5 1.8 collective-permute-start.6
  189.9 4.2 %all-to-all-start.3 = ((f32[8,32,128]{2,1,0:T(8,128)}), f32[8,32,128]{2,1,0:T(8,128)S(1)}, u32[]{:S(2)}, u32[]{:S(2)}) async-start(f32[8,32,128]{2,1,0:T(8,128)} %broadcast_in_dim.8), calls=%async_computation.3 | async-start | bytes 262144 | tf_op jit(solution)/shard_map/all_to_all | solution.py:376
  194.1 1.6 broadcast.3.clone
  196.5 1.6 all-to-all-done.3
  198.9 1.9 constant_dynamic-update-slice_fusion.2
  200.8 1.9 constant_dynamic-update-slice_fusion.1
  202.8 8.6 %collective-permute-done.11 = bf16[2,32,32,128]{3,2,1,0:T(8,128)(2,1)S(1)} collective-permute-done((bf16[2,32,32,128]{3,2,1,0:T(8,128)(2,1)S(1)}, bf16[2,32,32,128]{3,2,1,0:T(8,128)(2,1)S(1)}, u32[]{:S(2)}, u32[]{:S(2)}) %collective-permute-start.11) | collective-permute-done | bytes 524320 | tf_op jit(solution)/shard_map/ppermute | solution.py:362
  213.1 29.5 %collective-permute-done.7 = bf16[2,32,32,128]{3,2,1,0:T(8,128)(2,1)S(1)} collective-permute-done((bf16[2,32,32,128]{3,2,1,0:T(8,128)(2,1)}, bf16[2,32,32,128]{3,2,1,0:T(8,128)(2,1)S(1)}, u32[]{:S(2)}, u32[]{:S(2)}) %collective-permute-start.7) | collective-permute-done | bytes 524320 | tf_op jit(solution)/shard_map/ppermute | solution.py:362
  243.5 10.7 %collective-permute-done.8 = bf16[2,32,32,128]{3,2,1,0:T(8,128)(2,1)S(1)} collective-permute-done((bf16[2,32,32,128]{3,2,1,0:T(8,128)(2,1)S(1)}, bf16[2,32,32,128]{3,2,1,0:T(8,128)(2,1)S(1)}, u32[]{:S(2)}, u32[]{:S(2)}) %collective-permute-start.8) | collective-permute-done | bytes 524320 | tf_op jit(solution)/shard_map/ppermute | solution.py:362
  (97 shorter events, 32.1 us)
Async XLA Ops:
  0.6 6.2 %copy-start.3 = (bf16[2,128,32,128]{3,2,1,0:T(8,128)(2,1)S(1)}, bf16[2,128,32,128]{3,2,1,0:T(8,128)(2,1)}, u32[]{:S(2)}) copy-start(bf16[2,128,32,128]{3,2,1,0:T(8,128)(2,1)} %own_ref.3) | copy-start | bytes 6291460
  3.3 8.2 %copy-start.28 = (f32[2,128,128]{2,1,0:T(8,128)S(1)}, f32[2,128,128]{2,1,0:T(8,128)}, u32[]{:S(2)}) copy-start(f32[2,128,128]{2,1,0:T(8,128)} %param.10) | copy-start | bytes 393220
  3.4 8.2 %copy-start.29 = (f32[128,128]{1,0:T(8,128)S(1)}, f32[128,128]{1,0:T(8,128)}, u32[]{:S(2)}) copy-start(f32[128,128]{1,0:T(8,128)} %param.11) | copy-start | bytes 196612
  3.4 23.6 %collective-permute-start = (bf16[2,32,32,128]{3,2,1,0:T(8,128)(2,1)}, bf16[2,32,32,128]{3,2,1,0:T(8,128)(2,1)}, u32[]{:S(2)}, u32[]{:S(2)}) collective-permute-start(bf16[2,32,32,128]{3,2,1,0:T(8,128)(2,1)} %get-tuple-element.88), channel_id=1, source_target_pairs={{0,1},{1,0},{2,3},{3,2},{4,5},{5,4},{6,7},{7,6},{8,9},{9,8},{10,11... | collective-permute-start | bytes 1572872 | tf_op jit(solution)/shard_map/ppermute | solution.py:362
  3.8 37.7 %collective-permute-start.1 = (bf16[2,32,32,128]{3,2,1,0:T(8,128)(2,1)}, bf16[2,32,32,128]{3,2,1,0:T(8,128)(2,1)}, u32[]{:S(2)}, u32[]{:S(2)}) collective-permute-start(bf16[2,32,32,128]{3,2,1,0:T(8,128)(2,1)} %get-tuple-element.87), channel_id=1, source_target_pairs={{0,2},{1,3},{2,0},{3,1},{4,6},{5,7},{6,4},{7,5},{8,10},{9,11},{10,... | collective-permute-start | bytes 1572872 | tf_op jit(solution)/shard_map/ppermute | solution.py:362
  6.4 69.8 %collective-permute-start.2 = (bf16[2,32,32,128]{3,2,1,0:T(8,128)(2,1)}, bf16[2,32,32,128]{3,2,1,0:T(8,128)(2,1)}, u32[]{:S(2)}, u32[]{:S(2)}) collective-permute-start(bf16[2,32,32,128]{3,2,1,0:T(8,128)(2,1)} %get-tuple-element.86), channel_id=1, source_target_pairs={{0,3},{1,2},{2,1},{3,0},{4,7},{5,6},{6,5},{7,4},{8,11},{9,10},{10,... | collective-permute-start | bytes 1572872 | tf_op jit(solution)/shard_map/ppermute | solution.py:362
  8.0 82.2 %collective-permute-start.3 = (bf16[2,32,32,128]{3,2,1,0:T(8,128)(2,1)}, bf16[2,32,32,128]{3,2,1,0:T(8,128)(2,1)S(1)}, u32[]{:S(2)}, u32[]{:S(2)}) collective-permute-start(bf16[2,32,32,128]{3,2,1,0:T(8,128)(2,1)} %get-tuple-element.85), channel_id=1, source_target_pairs={{0,1},{1,0},{2,3},{3,2},{4,5},{5,4},{6,7},{7,6},{8,9},{9,8},{10,11... | collective-permute-start | bytes 1572872 | tf_op jit(solution)/shard_map/ppermute | solution.py:362
  9.4 80.8 %collective-permute-start.4 = (bf16[2,32,32,128]{3,2,1,0:T(8,128)(2,1)}, bf16[2,32,32,128]{3,2,1,0:T(8,128)(2,1)S(1)}, u32[]{:S(2)}, u32[]{:S(2)}) collective-permute-start(bf16[2,32,32,128]{3,2,1,0:T(8,128)(2,1)} %get-tuple-element.84), channel_id=1, source_target_pairs={{0,2},{1,3},{2,0},{3,1},{4,6},{5,7},{6,4},{7,5},{8,10},{9,11},{10,... | collective-permute-start | bytes 1572872 | tf_op jit(solution)/shard_map/ppermute | solution.py:362
  16.1 67.1 %copy-start.25 = (bf16[256,256]{1,0:T(8,128)(2,1)}, bf16[256,256]{1,0:T(8,128)(2,1)S(1)}, u32[]{:S(2)}) copy-start(bf16[256,256]{1,0:T(8,128)(2,1)S(1)} %get-tuple-element.45.low_ref) | copy-start | bytes 393220
  26.9 70.3 %collective-permute-start.5 = (bf16[2,32,32,128]{3,2,1,0:T(8,128)(2,1)}, bf16[2,32,32,128]{3,2,1,0:T(8,128)(2,1)}, u32[]{:S(2)}, u32[]{:S(2)}) collective-permute-start(bf16[2,32,32,128]{3,2,1,0:T(8,128)(2,1)} %get-tuple-element.83), channel_id=1, source_target_pairs={{0,3},{1,2},{2,1},{3,0},{4,7},{5,6},{6,5},{7,4},{8,11},{9,10},{10,... | collective-permute-start | bytes 1572872 | tf_op jit(solution)/shard_map/ppermute | solution.py:362
  30.5 4.1 %copy-start.27 = (bf16[2,128,32,128]{3,2,1,0:T(8,128)(2,1)S(1)}, bf16[2,128,32,128]{3,2,1,0:T(8,128)(2,1)}, u32[]{:S(2)}) copy-start(bf16[2,128,32,128]{3,2,1,0:T(8,128)(2,1)} %param.8) | copy-start | bytes 6291460
  76.1 1.6 copy-start
  77.7 1.6 copy-start.2
  79.3 3.8 %copy-start.1 = (bf16[32,8,32,128]{3,1,2,0:T(8,128)(2,1)S(1)}, bf16[32,8,32,128]{3,1,2,0:T(8,128)(2,1)}, u32[]{:S(2)}) copy-start(bf16[32,8,32,128]{3,1,2,0:T(8,128)(2,1)} %copy.19) | copy-start | bytes 6291460
  83.2 14.1 %copy-start.4 = (bf16[2,128,32,128]{3,2,1,0:T(8,128)(2,1)S(1)}, bf16[2,128,32,128]{3,2,1,0:T(8,128)(2,1)}, u32[]{:S(2)}) copy-start(bf16[2,128,32,128]{3,2,1,0:T(8,128)(2,1)} %own_ref.3) | copy-start | bytes 6291460
  87.6 1.3 copy-start.19
  88.9 1.3 copy-start.21
  90.2 11.1 %copy-start.23 = (f32[256,256]{1,0:T(8,128)}, f32[256,256]{1,0:T(8,128)S(1)}, u32[]{:S(2)}) copy-start(f32[256,256]{1,0:T(8,128)S(1)} %get-tuple-element.57.refs_0_) | copy-start | bytes 786436
  101.3 1.3 copy-start.11
  102.6 15.5 %all-to-all-start = ((f32[32,1,128]{2,1,0:T(1,128)}), f32[32,1,128]{2,1,0:T(1,128)S(1)}, u32[]{:S(2)}, u32[]{:S(2)}) async-start(f32[32,1,128]{2,1,0:T(1,128)} %get-tuple-element.54), calls=%async_computation | async-start | bytes 32768 | tf_op jit(solution)/shard_map/all_to_all | solution.py:434
  107.6 1.6 copy-start.12
  109.2 0.9 copy-start.24
  110.2 0.9 copy-start.26
  115.5 1.3 copy-start.15
  116.8 1.3 copy-start.17
  118.1 11.3 %copy-start.20 = (bf16[256,4096]{1,0:T(8,128)(2,1)S(1)}, bf16[256,4096]{1,0:T(8,128)(2,1)}, u32[]{:S(2)}) copy-start(bf16[256,4096]{1,0:T(8,128)(2,1)} %copy-done.19) | copy-start | bytes 6291460
  123.6 20.2 %all-to-all-start.1 = ((f32[32,1,128]{2,1,0:T(1,128)}), f32[32,1,128]{2,1,0:T(1,128)S(1)}, u32[]{:S(2)}, u32[]{:S(2)}) async-start(f32[32,1,128]{2,1,0:T(1,128)} %get-tuple-element.61), calls=%async_computation.1 | async-start | bytes 32768 | tf_op jit(solution)/shard_map/all_to_all | solution.py:438
  129.4 1.6 copy-start.22
  131.0 7.0 %copy-start.16 = (bf16[256,4096]{1,0:T(8,128)(2,1)S(1)}, bf16[256,4096]{1,0:T(8,128)(2,1)}, u32[]{:S(2)}) copy-start(bf16[256,4096]{1,0:T(8,128)(2,1)} %copy-done.15) | copy-start | bytes 6291460
  131.0 7.0 %copy-start.18 = (bf16[256,4096]{1,0:T(8,128)(2,1)S(1)}, bf16[256,4096]{1,0:T(8,128)(2,1)}, u32[]{:S(2)}) copy-start(bf16[256,4096]{1,0:T(8,128)(2,1)} %copy-done.17) | copy-start | bytes 6291460
  135.4 1.4 copy-start.5
  136.8 1.3 copy-start.7
  142.5 1.3 copy-start.9
  150.5 20.2 %all-to-all-start.2 = ((f32[8,32,128]{2,1,0:T(8,128)}), f32[8,32,128]{2,1,0:T(8,128)S(1)}, u32[]{:S(2)}, u32[]{:S(2)}) async-start(f32[8,32,128]{2,1,0:T(8,128)} %bitcast.10), calls=%async_computation.2 | async-start | bytes 262144 | tf_op jit(solution)/shard_map/all_to_all | solution.py:368
  154.7 1.6 copy-start.6
  156.3 5.6 %copy-start.10 = (bf16[256,4096]{1,0:T(8,128)(2,1)S(1)}, bf16[256,4096]{1,0:T(8,128)(2,1)}, u32[]{:S(2)}) copy-start(bf16[256,4096]{1,0:T(8,128)(2,1)} %copy-done.9) | copy-start | bytes 6291460
  158.8 39.3 %collective-permute-start.9 = (bf16[2,32,32,128]{3,2,1,0:T(8,128)(2,1)}, bf16[2,32,32,128]{3,2,1,0:T(8,128)(2,1)}, u32[]{:S(2)}, u32[]{:S(2)}) collective-permute-start(bf16[2,32,32,128]{3,2,1,0:T(8,128)(2,1)} %get-tuple-element.79), channel_id=1, source_target_pairs={{0,1},{1,0},{2,3},{3,2},{4,5},{5,4},{6,7},{7,6},{8,9},{9,8},{10,11... | collective-permute-start | bytes 1572872 | tf_op jit(solution)/shard_map/ppermute | solution.py:362
  159.4 41.4 %collective-permute-start.10 = (bf16[2,32,32,128]{3,2,1,0:T(8,128)(2,1)}, bf16[2,32,32,128]{3,2,1,0:T(8,128)(2,1)}, u32[]{:S(2)}, u32[]{:S(2)}) collective-permute-start(bf16[2,32,32,128]{3,2,1,0:T(8,128)(2,1)} %get-tuple-element.80), channel_id=1, source_target_pairs={{0,2},{1,3},{2,0},{3,1},{4,6},{5,7},{6,4},{7,5},{8,10},{9,11},{10,... | collective-permute-start | bytes 1572872 | tf_op jit(solution)/shard_map/ppermute | solution.py:362
  163.1 1.9 copy-start.8
  170.6 14.3 %collective-permute-start.12 = (f32[32,128]{1,0:T(8,128)S(1)}, f32[32,128]{1,0:T(8,128)S(1)}, u32[]{:S(2)}, u32[]{:S(2)}) collective-permute-start(f32[32,128]{1,0:T(8,128)S(1)} %reduce_sum.19), channel_id=1, source_target_pairs={{0,1},{1,0},{2,3},{3,2},{4,5},{5,4},{6,7},{7,6},{8,9},{9,8},{10,11... | collective-permute-start | bytes 49160 | tf_op jit(solution)/shard_map/ppermute | solution.py:362
  172.2 14.3 %collective-permute-start.13 = (f32[32,128]{1,0:T(8,128)S(1)}, f32[32,128]{1,0:T(8,128)S(1)}, u32[]{:S(2)}, u32[]{:S(2)}) collective-permute-start(f32[32,128]{1,0:T(8,128)S(1)} %reduce_sum.19), channel_id=1, source_target_pairs={{0,2},{1,3},{2,0},{3,1},{4,6},{5,7},{6,4},{7,5},{8,10},{9,11},{10,... | collective-permute-start | bytes 49160 | tf_op jit(solution)/shard_map/ppermute | solution.py:362
  172.7 15.6 %collective-permute-start.14 = (f32[32,128]{1,0:T(8,128)S(1)}, f32[32,128]{1,0:T(8,128)S(1)}, u32[]{:S(2)}, u32[]{:S(2)}) collective-permute-start(f32[32,128]{1,0:T(8,128)S(1)} %reduce_sum.19), channel_id=1, source_target_pairs={{0,3},{1,2},{2,1},{3,0},{4,7},{5,6},{6,5},{7,4},{8,11},{9,10},{10,... | collective-permute-start | bytes 49160 | tf_op jit(solution)/shard_map/ppermute | solution.py:362
  185.0 13.1 %copy-start.14 = (bf16[2,32,32,128]{3,2,1,0:T(8,128)(2,1)S(1)}, bf16[2,32,32,128]{3,2,1,0:T(8,128)(2,1)}, u32[]{:S(2)}) copy-start(bf16[2,32,32,128]{3,2,1,0:T(8,128)(2,1)} %copy-done.13) | copy-start | bytes 1572868
  185.0 26.3 %collective-permute-start.11 = (bf16[2,32,32,128]{3,2,1,0:T(8,128)(2,1)S(1)}, bf16[2,32,32,128]{3,2,1,0:T(8,128)(2,1)S(1)}, u32[]{:S(2)}, u32[]{:S(2)}) collective-permute-start(bf16[2,32,32,128]{3,2,1,0:T(8,128)(2,1)S(1)} %get-tuple-element.81), channel_id=1, source_target_pairs={{0,3},{1,2},{2,1},{3,0},{4,7},{5,6},{6,5},{7,4},{8,11},{9,10},{10,... | collective-permute-start | bytes 1572872 | tf_op jit(solution)/shard_map/ppermute | solution.py:362
  186.5 25.7 %collective-permute-start.6 = (bf16[2,32,32,128]{3,2,1,0:T(8,128)(2,1)}, bf16[2,32,32,128]{3,2,1,0:T(8,128)(2,1)S(1)}, u32[]{:S(2)}, u32[]{:S(2)}) collective-permute-start(bf16[2,32,32,128]{3,2,1,0:T(8,128)(2,1)} %get-tuple-element.73), channel_id=1, source_target_pairs={{0,1},{1,0},{2,3},{3,2},{4,5},{5,4},{6,7},{7,6},{8,9},{9,8},{10,11... | collective-permute-start | bytes 1572872 | tf_op jit(solution)/shard_map/ppermute | solution.py:362
  188.2 54.4 %collective-permute-start.7 = (bf16[2,32,32,128]{3,2,1,0:T(8,128)(2,1)}, bf16[2,32,32,128]{3,2,1,0:T(8,128)(2,1)S(1)}, u32[]{:S(2)}, u32[]{:S(2)}) collective-permute-start(bf16[2,32,32,128]{3,2,1,0:T(8,128)(2,1)} %get-tuple-element.74), channel_id=1, source_target_pairs={{0,2},{1,3},{2,0},{3,1},{4,6},{5,7},{6,4},{7,5},{8,10},{9,11},{10,... | collective-permute-start | bytes 1572872 | tf_op jit(solution)/shard_map/ppermute | solution.py:362
  189.9 8.2 %all-to-all-start.3 = ((f32[8,32,128]{2,1,0:T(8,128)}), f32[8,32,128]{2,1,0:T(8,128)S(1)}, u32[]{:S(2)}, u32[]{:S(2)}) async-start(f32[8,32,128]{2,1,0:T(8,128)} %broadcast_in_dim.8), calls=%async_computation.3 | async-start | bytes 262144 | tf_op jit(solution)/shard_map/all_to_all | solution.py:376
  198.1 56.2 %collective-permute-start.8 = (bf16[2,32,32,128]{3,2,1,0:T(8,128)(2,1)S(1)}, bf16[2,32,32,128]{3,2,1,0:T(8,128)(2,1)S(1)}, u32[]{:S(2)}, u32[]{:S(2)}) collective-permute-start(bf16[2,32,32,128]{3,2,1,0:T(8,128)(2,1)S(1)} %copy-done.14), channel_id=1, source_target_pairs={{0,3},{1,2},{2,1},{3,0},{4,7},{5,6},{6,5},{7,4},{8,11},{9,10},{10,... | collective-permute-start | bytes 1572872 | tf_op jit(solution)/shard_map/ppermute | solution.py:362
  (1 other events, 0.8 us)
where the time goes:
time: 257 us; the launch traced here: 256 us
  waiting for transfers between devices  112 us (44%)
  Pallas kernels  49.6 us (19%)
  local copies, waits for them, and re-layouts  47.5 us (18%)
  starting transfers between devices  40.4 us (16%)
  matrix products  3.98 us (2%)
    ppermute x15, waiting for transfers between devices, swap(): lax.ppermute(value, name, [(j, j ^ r) for j in range(lax.axis_size(name))])  111 us
    pallas_call x14, Pallas kernels, call(): pl.pallas_call(body, out_shape=[jax.ShapeDtypeStruct(shape, kind) for sha...  49.6 us
    unnamed x66, local copies, waits for them, and re-layouts  30.6 us
    ppermute x15, starting transfers between devices, swap(): lax.ppermute(value, name, [(j, j ^ r) for j in range(lax.axis_size(name))])  21.2 us
    all_to_all x2, starting transfers between devices, per_device(): levels = lax.all_to_all(part, ('hist', 'col'), 0, 0, tiled=True)  10.8 us
    dynamic_update_slice x8, local copies, waits for them, and re-layouts, return_pieces(): out = lax.dynamic_update_slice_in_dim(out, moved, (me ^ r) * count, axis=1)  9.15 us
  transfers between devices with their start and end apart: 19, of which 9 were waited for; matrix products, arithmetic and copies ran while one was open for 11% of the time, Pallas kernels for 13%

commit v1 on v0

--- a/solution.py
+++ b/solution.py
@@ -108,20 +108,31 @@
 
 
 IN_VMEM = pl.BlockSpec(memory_space=pltpu.VMEM)
-GRANT = pltpu.CompilerParams(vmem_limit_bytes=8 * 2**20)
-
-
-def call(body, outs, args, cost_estimate, scratch=(), scalars=0):
-    specs = [pl.BlockSpec(memory_space=pltpu.SMEM)] * scalars + [IN_VMEM] * (len(args) - scalars)
+IN_HBM = pl.BlockSpec(memory_space=pl.ANY)
+
+
+def call(body, outs, args, cost_estimate, scratch=(), scalars=0, streamed=(), streamed_outs=(), grant=8):
+    specs = [pl.BlockSpec(memory_space=pltpu.SMEM)] * scalars
+    specs += [IN_HBM if i in streamed else IN_VMEM for i in range(scalars, len(args))]
     return pl.pallas_call(
         body,
-        out_shape=[jax.ShapeDtypeStruct(shape, kind) for shape, kind in outs],
+        out_shape=[
+            pltpu.HBM(shape, kind) if i in streamed_outs else jax.ShapeDtypeStruct(shape, kind)
+            for i, (shape, kind) in enumerate(outs)
+        ],
         in_specs=specs,
-        out_specs=[IN_VMEM] * len(outs),
+        out_specs=[IN_HBM if i in streamed_outs else IN_VMEM for i in range(len(outs))],
         scratch_shapes=list(scratch),
         cost_estimate=cost_estimate,
-        compiler_params=GRANT,
+        compiler_params=pltpu.CompilerParams(vmem_limit_bytes=grant * 2**20 if grant else None),
     )(*args)
+
+
+def stream(outside, inside, semaphores, base, group, width, inward):
+    lanes = lanes_of(base, 0, width)
+    ends = (outside.at[:, lanes], inside.at[:, lanes])
+    source, target = ends if inward else ends[::-1]
+    return pltpu.make_async_copy(source, target, semaphores.at[group])
 
 
 def solve(levels, hamiltonian, rho=None, later=None):
@@ -177,7 +188,7 @@
 
 def each_group(total_width, width, body):
     def step(g, carry):
-        body(pl.multiple_of(g * width, width))
+        body(pl.multiple_of(g * width, width), g)
         return carry
 
     lax.fori_loop(0, total_width // width, step, 0)
@@ -200,9 +211,9 @@
 def now_kernel(parts, last, me_ref, row_ref, own_ref, *refs):
     pieces, refs = refs[: parts - 1], refs[parts - 1 :]
     if last:
-        before_ref, known_ref, col_out, rho_out, level_out, acc, sig, place = refs
+        before_ref, known_ref, col_hbm, rho_out, level_out, acc, sig, place, col_out, sent = refs
     else:
-        col_out, acc, sig, place = refs
+        col_hbm, acc, sig, place, col_out, sent = refs
     _, count, block, times = pieces[0].shape
     width = sig.shape[1]
     group = width // times
@@ -210,7 +221,7 @@
     direct = place.dtype == col_out.dtype
     acc[...] = jnp.zeros_like(acc)
 
-    def body(base):
+    def body(base, g):
         first = lax.div(base, times)
         for r in range(parts):
             source = lax.bitwise_xor(me_ref[0], r) * block
@@ -227,32 +238,62 @@
                         place[rows, pl.ds(k * times, times)] = value.astype(place.dtype)
         if not direct:
             col_out[:, lanes_of(base, 0, width)] = place[...].astype(col_out.dtype)
+        stream(col_hbm, col_out, sent, base, g, width, False).start()
         sigma_into(sig, row_ref, col_out, base, 16, min(SPAN, width))
         acc[...] += overlap(sig[...], col_out[:, lanes_of(base, 0, width)])
 
     each_group(col_out.shape[1], width, body)
+    each_group(col_out.shape[1], width, lambda base, g: stream(col_hbm, col_out, sent, base, g, width, False).wait())
     if last:
         real = finish_sum(acc, before_ref, known_ref, rho_out, step_length)
         spread_rows(level_out, diagonal_row(real))
 
 
-def later_kernel(last, row_ref, col_ref, low_ref, *refs):
+def later_kernel(last, row_hbm, col_hbm, low_ref, *refs):
     if last:
-        before_ref, row_out, col_out, sum_out, acc, sig = refs
+        before_ref, row_to, col_to, sum_out, acc, *refs = refs
     else:
-        row_out, col_out, acc, sig = refs
-    width = sig.shape[1]
+        row_to, col_to, acc, *refs = refs
+    sig, row_ref, col_ref, row_out, col_out, row_came, col_came, row_went, col_went = refs
+    total_width, width = row_ref.shape[1], sig.shape[1]
+
+    def loads(base, g):
+        return (
+            stream(row_hbm, row_ref, row_came, base, g, width, True),
+            stream(col_hbm, col_ref, col_came, base, g, width, True),
+        )
+
+    def stores(base, g):
+        return (
+            stream(row_to, row_out, row_went, base, g, width, False),
+            stream(col_to, col_out, col_went, base, g, width, False),
+        )
+
+    def start(base, g):
+        for copy in loads(base, g):
+            copy.start()
+
+    def wait(base, g):
+        for copy in stores(base, g):
+            copy.wait()
+
+    each_group(total_width, width, start)
     acc[...] = jnp.zeros_like(acc)
 
-    def body(base):
+    def body(base, g):
+        for copy in loads(base, g):
+            copy.wait()
         advance_into(row_out, row_form(low_ref[...]), row_ref, base, width)
         advance_into(col_out, low_ref[...], col_ref, base, width)
+        for copy in stores(base, g):
+            copy.start()
         sigma_into(sig, row_out, col_out, base, 16, min(SPAN, width))
         acc[...] += overlap(sig[...], col_out[:, lanes_of(base, 0, width)])
 
-    each_group(col_out.shape[1], width, body)
+    each_group(total_width, width, body)
     if last:
         finish_sum(acc, before_ref, None, sum_out, step_length)
+    each_group(total_width, width, wait)
 
 
 def finish_kernel(left_ref, unit_ref, later_ref, unit_last_ref, last_ref, rho_ref):
@@ -275,7 +316,7 @@
 
 def row_kernel(width, row_ref, low_ref, row_out):
     low = row_form(low_ref[...])
-    each_group(row_ref.shape[1], width, lambda base: advance_into(row_out, low, row_ref, base, width))
+    each_group(row_ref.shape[1], width, lambda base, g: advance_into(row_out, low, row_ref, base, width))
 
 
 def last_kernel(parts, me_ref, col_ref, low_ref, *refs):
@@ -285,7 +326,7 @@
     size = moved.shape[0] // 2
     low = low_ref[...]
 
-    def body(base):
+    def body(base, g):
         first = lax.div(base, times)
         advance_into(moved, low, col_ref, base, width, local=True)
         for r in range(parts):
@@ -316,25 +357,28 @@
     width = min(GROUP, count) * times
     square, history = ((2 * size, 2 * size), jnp.float32), (row.shape, jnp.bfloat16)
     args = (me, row, own, *pieces)
-    place = pltpu.VMEM((2 * size, width), place_type(block))
-    sig = pltpu.VMEM((2 * size, width), jnp.bfloat16)
+    scratch = sum_scratch(size, width)
+    scratch += [pltpu.VMEM((2 * size, width), place_type(block)), pltpu.VMEM(row.shape, jnp.bfloat16)]
+    scratch += [pltpu.SemaphoreType.DMA((row.shape[1] // width,))]
     body = functools.partial(now_kernel, len(pieces) + 1, before is not None)
     if before is None:
-        return call(body, [history, square], args, cost(4, 2), [sig, place], 1)
-    outs = [history, ((2, size, size), jnp.float32), ((devices, 1, size), jnp.float32)]
-    scratch = sum_scratch(size, width) + [place]
-    return call(body, outs, args + (before, known), cost(4, 2), scratch, 1)
+        outs, scratch = [history, square], scratch[1:]
+    else:
+        outs, args = [history, ((2, size, size), jnp.float32), ((devices, 1, size), jnp.float32)], args + (before, known)
+    return call(body, outs, args, cost(4, 2), scratch, 1, streamed_outs=(0,))
 
 
 def later_step(row, col, low, width, before=None):
     double = row.shape[0]
     square, history = ((double, double), jnp.float32), (row.shape, jnp.bfloat16)
     body = functools.partial(later_kernel, before is not None)
+    scratch = sum_scratch(double // 2, width) + [pltpu.VMEM(row.shape, jnp.bfloat16)] * 4
+    scratch += [pltpu.SemaphoreType.DMA((row.shape[1] // width,))] * 4
     if before is None:
-        scratch = [pltpu.VMEM((double, width), jnp.bfloat16)]
-        return call(body, [history, history, square], (row, col, low), cost(4, 3), scratch)
-    outs = [history, history, ((2, double // 2, double // 2), jnp.float32)]
-    return call(body, outs, (row, col, low, before), cost(4, 3), sum_scratch(double // 2, width))
+        outs, args, scratch = [history, history, square], (row, col, low), scratch[1:]
+    else:
+        outs, args = [history, history, ((2, double // 2, double // 2), jnp.float32)], (row, col, low, before)
+    return call(body, outs, args, cost(4, 3), scratch, 0, (0, 1), (0, 1), None)
 
 
 def row_step(row, low, width):
@@ -437,10 +481,11 @@
 
     levels = lax.all_to_all(part, ("hist", "col"), 0, 0, tiled=True)
     less, cols_great, minus = later_step(less, cols_great, low, width)
+    low_last, unit_last = solve(levels, symmetric)
+
+    great_out = return_pieces(last_step(me, cols_great, low_last, parts, count, times))
     great, cols_less, last = later_step(great, cols_less, low, width, minus)
-    low, unit_last = solve(levels, symmetric)
-
-    great_out = return_pieces(last_step(me, cols_great, low, parts, count, times))
+    low = low_last
     args = (left, unit, later, unit_last, last)
     estimate = pl.CostEstimate(flops=500_000_000, bytes_accessed=1_000_000, transcendentals=0)
     rho = call(finish_kernel, [(density.shape, jnp.float32)], args, estimate)[0]

time: 257 us -> 256 us (level)
  Pallas kernels: 49.6 us -> 63.7 us
  local copies, waits for them, and re-layouts: 47.5 us -> 34.2 us
    pallas_call x14, Pallas kernels: 49.6 us -> 63.7 us  [call(): pl.pallas_call(body, out_shape=[pltpu.HBM(shape, kind) if i in streamed_o...]
    unnamed x66 -> x52, local copies, waits for them, and re-layouts: 30.6 us -> 17.3 us
  transfers between devices with their start and end apart: 19 -> 19, of which waited for: 9 -> 9; matrix products, arithmetic and copies ran while one was open for 11% -> 9% of each run, Pallas kernels for 13% -> 18%
where the time goes in v1:
time: 256 us
  waiting for transfers between devices  114 us (45%)
  Pallas kernels  63.7 us (25%)
  starting transfers between devices  40.4 us (16%)
  local copies, waits for them, and re-layouts  34.2 us (13%)
    ppermute x15, waiting for transfers between devices, swap(): lax.ppermute(value, name, [(j, j ^ r) for j in range(lax.axis_size(name))])  113 us
    pallas_call x14, Pallas kernels, call(): pl.pallas_call(body, out_shape=[pltpu.HBM(shape, kind) if i in streamed_o...  63.7 us
    ppermute x15, starting transfers between devices, swap(): lax.ppermute(value, name, [(j, j ^ r) for j in range(lax.axis_size(name))])  21.2 us
    unnamed x52, local copies, waits for them, and re-layouts  17.3 us
    all_to_all x2, starting transfers between devices, per_device(): levels = lax.all_to_all(part, ('hist', 'col'), 0, 0, tiled=True)  10.8 us
    dynamic_update_slice x8, local copies, waits for them, and re-layouts, return_pieces(): out = lax.dynamic_update_slice_in_dim(out, moved, (me ^ r) * count, axis=1)  9.15 us
  transfers between devices with their start and end apart: 19, of which 9 were waited for; matrix products, arithmetic and copies ran while one was open for 9% of the time, Pallas kernels for 18%

profile of v1, /device:TPU:10, one launch (start us, length us, event | category | flops | bytes accessed | tf_op | source)
XLA Modules:
  0.0 255.6 jit_solution(8346540858360709298)
XLA Ops:
  0.7 2.7 %constant_dynamic-slice_fusion.3 = (bf16[2,32,32,128]{3,2,1,0:T(8,128)(2,1)}, bf16[2,32,32,128]{3,2,1,0:T(8,128)(2,1)}, bf16[2,32,32,128]{3,2,1,0:T(8,128)(2,1)}) fusion(bf16[2,128,32,128]{3,2,1,0:T(8,128)(2,1)} %own_ref.2, s32[]{:T(128)S(6)} %select_n.14, s32[]{:T(128)S(6)} %select_n.13, s32[]{:T(128)S(6)} %select_n.12), kind=kLoop, calls=%fused_computation.49 | loop fusion | bytes 3145740 | tf_op jit(solution)/shard_map/dynamic_slice | solution.py:442
  3.8 2.6 %collective-permute-start.1 = (bf16[2,32,32,128]{3,2,1,0:T(8,128)(2,1)}, bf16[2,32,32,128]{3,2,1,0:T(8,128)(2,1)}, u32[]{:S(2)}, u32[]{:S(2)}) collective-permute-start(bf16[2,32,32,128]{3,2,1,0:T(8,128)(2,1)} %get-tuple-element.87), channel_id=1, source_target_pairs={{0,2},{1,3},{2,0},{3,1},{4,6},{5,7},{6,4},{7,5},{8,10},{9,11},{10,... | collective-permute-start | bytes 1572872 | tf_op jit(solution)/shard_map/ppermute | solution.py:406
  6.8 1.2 constant_dynamic-slice_fusion
  8.0 1.3 collective-permute-start.3
  9.4 2.1 collective-permute-start.4
  11.7 4.4 %shard_map.102 = (bf16[256,256]{1,0:T(8,128)(2,1)S(1)}, f32[2,128,128]{2,1,0:T(8,128)S(1)}) custom-call(f32[1,1,128]{2,1,0:T(1,128)S(1)} %bitcast.68, f32[128,128]{1,0:T(8,128)S(1)} %fusion.14.ham_ref), custom_call_target="tpu_custom_call" | custom-call | flops 4000000000 | bytes 1000000 | tf_op jit(solution)/shard_map/pallas_call | solution.py:117
  17.5 9.4 %collective-permute-done.refs_0_ = bf16[2,32,32,128]{3,2,1,0:T(8,128)(2,1)} collective-permute-done((bf16[2,32,32,128]{3,2,1,0:T(8,128)(2,1)}, bf16[2,32,32,128]{3,2,1,0:T(8,128)(2,1)}, u32[]{:S(2)}, u32[]{:S(2)}) %collective-permute-start) | collective-permute-done | bytes 524320 | tf_op jit(solution)/shard_map/ppermute | solution.py:406
  26.9 2.7 %collective-permute-start.5 = (bf16[2,32,32,128]{3,2,1,0:T(8,128)(2,1)}, bf16[2,32,32,128]{3,2,1,0:T(8,128)(2,1)}, u32[]{:S(2)}, u32[]{:S(2)}) collective-permute-start(bf16[2,32,32,128]{3,2,1,0:T(8,128)(2,1)} %get-tuple-element.83), channel_id=1, source_target_pairs={{0,3},{1,2},{2,1},{3,0},{4,7},{5,6},{6,5},{7,4},{8,11},{9,10},{10,... | collective-permute-start | bytes 1572872 | tf_op jit(solution)/shard_map/ppermute | solution.py:406
  29.9 4.0 %copy.19 = bf16[32,8,32,128]{3,1,2,0:T(8,128)(2,1)} copy(bf16[32,8,32,128]{3,2,1,0:T(8,128)(2,1)} %bitcast.69) | data formatting | bytes 4194304
  35.2 6.3 %collective-permute-done.1.refs_1_ = bf16[2,32,32,128]{3,2,1,0:T(8,128)(2,1)} collective-permute-done((bf16[2,32,32,128]{3,2,1,0:T(8,128)(2,1)}, bf16[2,32,32,128]{3,2,1,0:T(8,128)(2,1)}, u32[]{:S(2)}, u32[]{:S(2)}) %collective-permute-start.1) | collective-permute-done | bytes 524320 | tf_op jit(solution)/shard_map/ppermute | solution.py:406
  41.5 34.6 %collective-permute-done.2.refs_2_ = bf16[2,32,32,128]{3,2,1,0:T(8,128)(2,1)} collective-permute-done((bf16[2,32,32,128]{3,2,1,0:T(8,128)(2,1)}, bf16[2,32,32,128]{3,2,1,0:T(8,128)(2,1)}, u32[]{:S(2)}, u32[]{:S(2)}) %collective-permute-start.2) | collective-permute-done | bytes 524320 | tf_op jit(solution)/shard_map/ppermute | solution.py:406
  76.1 1.6 copy-done.1
  77.7 1.6 copy-done.2
  79.3 4.1 %shard_map.101 = (bf16[256,4096]{1,0:T(8,128)(2,1)}, f32[256,256]{1,0:T(8,128)S(1)}) custom-call(s32[1]{0:T(128)} %bitcast.me_ref, bf16[256,4096]{1,0:T(8,128)(2,1)S(1)} %bitcast.65, bf16[2,128,32,128]{3,2,1,0:T(8,128)(2,1)S(1)} %copy-done.2, bf16[2,32,32,128]{3,2,1,0:T(8,128)(2,1)} %collective-permute-done.refs_0_, ...), custom_call_target="tpu_custom_call" | custom-call | flops 1073741824 | bytes 8388608 | tf_op jit(solution)/shard_map/pallas_call | solution.py:117
  83.5 7.6 %shard_map.103 = (bf16[256,4096]{1,0:T(8,128)(2,1)}, bf16[256,4096]{1,0:T(8,128)(2,1)}, f32[256,256]{1,0:T(8,128)}) custom-call(bf16[256,4096]{1,0:T(8,128)(2,1)} %bitcast.64, bf16[256,4096]{1,0:T(8,128)(2,1)} %get-tuple-element.44.col_hbm, bf16[256,256]{1,0:T(8,128)(2,1)} %copy-done.18), custom_call_target="tpu_custom_call" | custom-call | flops 1610612736 | bytes 8388608 | tf_op jit(solution)/shard_map/pallas_call | solution.py:117
  91.2 6.1 %collective-permute-done.5.refs_2_ = bf16[2,32,32,128]{3,2,1,0:T(8,128)(2,1)} collective-permute-done((bf16[2,32,32,128]{3,2,1,0:T(8,128)(2,1)}, bf16[2,32,32,128]{3,2,1,0:T(8,128)(2,1)}, u32[]{:S(2)}, u32[]{:S(2)}) %collective-permute-start.5) | collective-permute-done | bytes 524320 | tf_op jit(solution)/shard_map/ppermute | solution.py:406
  97.3 1.6 copy-done.4
  98.8 4.5 %shard_map.104 = (bf16[256,4096]{1,0:T(8,128)(2,1)}, f32[2,128,128]{2,1,0:T(8,128)S(1)}, f32[32,1,128]{2,1,0:T(1,128)}) custom-call(s32[1]{0:T(128)} %bitcast.me_ref, bf16[256,4096]{1,0:T(8,128)(2,1)S(1)} %bitcast.62, bf16[2,128,32,128]{3,2,1,0:T(8,128)(2,1)S(1)} %copy-done.4, bf16[2,32,32,128]{3,2,1,0:T(8,128)(2,1)S(1)} %collective-permute-done.3.refs_0_, ...), custom_call_target="tpu_custom_call" | custom-call | flops 1073741824 | bytes 8388608 | tf_op jit(solution)/shard_map/pallas_call | solution.py:117
  104.0 5.0 %all-to-all-start = ((f32[32,1,128]{2,1,0:T(1,128)}), f32[32,1,128]{2,1,0:T(1,128)S(1)}, u32[]{:S(2)}, u32[]{:S(2)}) async-start(f32[32,1,128]{2,1,0:T(1,128)} %get-tuple-element.54), calls=%async_computation | async-start | bytes 32768 | tf_op jit(solution)/shard_map/all_to_all | solution.py:478
  109.0 7.8 %shard_map.105 = (bf16[256,4096]{1,0:T(8,128)(2,1)}, bf16[256,4096]{1,0:T(8,128)(2,1)}, f32[2,128,128]{2,1,0:T(8,128)}) custom-call(bf16[256,4096]{1,0:T(8,128)(2,1)} %bitcast.63, bf16[256,4096]{1,0:T(8,128)(2,1)} %get-tuple-element.56.col_hbm, bf16[256,256]{1,0:T(8,128)(2,1)} %copy-done.18, f32[256,256]{1,0:T(8,128)} %get-tuple-element.57.refs_0_), custom_call_target="tpu_custom_call" | custom-call | flops 1610612736 | bytes 8388608 | tf_op jit(solution)/shard_map/pallas_call | solution.py:117
  117.7 5.4 %shard_map.106 = (bf16[256,256]{1,0:T(8,128)(2,1)S(1)}, f32[2,128,128]{2,1,0:T(8,128)S(1)}, f32[2,128,128]{2,1,0:T(8,128)S(1)}, f32[32,1,128]{2,1,0:T(1,128)}) custom-call(f32[32,1,128]{2,1,0:T(1,128)S(1)} %all-to-all-done.levels_ref, f32[128,128]{1,0:T(8,128)S(1)} %copy-done.10, f32[2,128,128]{2,1,0:T(8,128)S(1)} %copy-done.14, f32[2,128,128]{2,1,0:T(8,128)S(1)} %copy-done.15), custom_call_target="tpu_custom_call" | custom-call | flops 4000000000 | bytes 1000000 | tf_op jit(solution)/shard_map/pallas_call | solution.py:117
  123.8 5.8 %all-to-all-start.1 = ((f32[32,1,128]{2,1,0:T(1,128)}), f32[32,1,128]{2,1,0:T(1,128)S(1)}, u32[]{:S(2)}, u32[]{:S(2)}) async-start(f32[32,1,128]{2,1,0:T(1,128)} %get-tuple-element.61), calls=%async_computation.1 | async-start | bytes 32768 | tf_op jit(solution)/shard_map/all_to_all | solution.py:482
  129.6 7.7 %shard_map.107 = (bf16[256,4096]{1,0:T(8,128)(2,1)}, bf16[256,4096]{1,0:T(8,128)(2,1)}, f32[256,256]{1,0:T(8,128)}) custom-call(bf16[256,4096]{1,0:T(8,128)(2,1)} %get-tuple-element.46.row_hbm, bf16[256,4096]{1,0:T(8,128)(2,1)} %get-tuple-element.47.col_hbm, bf16[256,256]{1,0:T(8,128)(2,1)} %copy-done.19), custom_call_target="tpu_custom_call" | custom-call | flops 1610612736 | bytes 8388608 | tf_op jit(solution)/shard_map/pallas_call | solution.py:117
  137.3 7.7 %shard_map.110 = (bf16[256,4096]{1,0:T(8,128)(2,1)}, bf16[256,4096]{1,0:T(8,128)(2,1)}, f32[2,128,128]{2,1,0:T(8,128)}) custom-call(bf16[256,4096]{1,0:T(8,128)(2,1)} %get-tuple-element.63.row_hbm, bf16[256,4096]{1,0:T(8,128)(2,1)} %get-tuple-element.64.col_hbm, bf16[256,256]{1,0:T(8,128)(2,1)} %copy-done.19, f32[256,256]{1,0:T(8,128)} %get-tuple-element.65.refs_0_), custom_call_target="tpu_custom_call" | custom-call | flops 1610612736 | bytes 8388608 | tf_op jit(solution)/shard_map/pallas_call | solution.py:117
  145.1 4.4 %shard_map.108 = (bf16[256,256]{1,0:T(8,128)(2,1)S(1)}, f32[2,128,128]{2,1,0:T(8,128)S(1)}) custom-call(f32[32,1,128]{2,1,0:T(1,128)S(1)} %all-to-all-done.1.levels_ref, f32[128,128]{1,0:T(8,128)S(1)} %copy-done.10), custom_call_target="tpu_custom_call" | custom-call | flops 4000000000 | bytes 1000000 | tf_op jit(solution)/shard_map/pallas_call | solution.py:117
  149.6 2.2 shard_map.111
  151.8 4.2 %all-to-all-start.2 = ((f32[8,32,128]{2,1,0:T(8,128)}), f32[8,32,128]{2,1,0:T(8,128)S(1)}, u32[]{:S(2)}, u32[]{:S(2)}) async-start(f32[8,32,128]{2,1,0:T(8,128)} %bitcast.10), calls=%async_computation.2 | async-start | bytes 262144 | tf_op jit(solution)/shard_map/all_to_all | solution.py:412
  156.0 2.6 %shard_map.114 = (bf16[2,32,32,128]{3,2,1,0:T(8,128)(2,1)S(1)}, bf16[2,32,32,128]{3,2,1,0:T(8,128)(2,1)}, bf16[2,32,32,128]{3,2,1,0:T(8,128)(2,1)}, bf16[2,32,32,128]{3,2,1,0:T(8,128)(2,1)S(1)}) custom-call(s32[1]{0:T(128)} %bitcast.me_ref, bf16[256,4096]{1,0:T(8,128)(2,1)S(1)} %copy-done.6, bf16[256,256]{1,0:T(8,128)(2,1)S(1)} %get-tuple-element.62.low_ref), custom_call_target="tpu_custom_call" | custom-call | flops 536870912 | bytes 4194304 | tf_op jit(solution)/shard_map/pallas_call | solution.py:117
  159.2 2.4 collective-permute-start.10
  161.6 1.3 shard_map.113
  162.9 1.8 copy.15
  164.8 1.3 shard_map.109
  166.1 1.8 copy.14
  167.9 1.6 broadcast.3.clone.1
  170.4 1.6 collective-permute-start.12
  172.5 1.5 collective-permute-start.14
  173.9 2.6 %shard_map.112 = (bf16[2,32,32,128]{3,2,1,0:T(8,128)(2,1)S(1)}, bf16[2,32,32,128]{3,2,1,0:T(8,128)(2,1)}, bf16[2,32,32,128]{3,2,1,0:T(8,128)(2,1)}, bf16[2,32,32,128]{3,2,1,0:T(8,128)(2,1)S(1)}) custom-call(s32[1]{0:T(128)} %bitcast.me_ref, bf16[256,4096]{1,0:T(8,128)(2,1)S(1)} %copy-done.5, bf16[256,256]{1,0:T(8,128)(2,1)S(1)} %get-tuple-element.62.low_ref), custom_call_target="tpu_custom_call" | custom-call | flops 536870912 | bytes 4194304 | tf_op jit(solution)/shard_map/pallas_call | solution.py:117
  177.4 7.4 %collective-permute-done.12 = f32[32,128]{1,0:T(8,128)S(1)} collective-permute-done((f32[32,128]{1,0:T(8,128)S(1)}, f32[32,128]{1,0:T(8,128)S(1)}, u32[]{:S(2)}, u32[]{:S(2)}) %collective-permute-start.12) | collective-permute-done | bytes 16416 | tf_op jit(solution)/shard_map/ppermute | solution.py:406
  184.8 1.5 collective-permute-start.11
  186.2 1.8 collective-permute-start.6
  189.6 4.2 %all-to-all-start.3 = ((f32[8,32,128]{2,1,0:T(8,128)}), f32[8,32,128]{2,1,0:T(8,128)S(1)}, u32[]{:S(2)}, u32[]{:S(2)}) async-start(f32[8,32,128]{2,1,0:T(8,128)} %broadcast_in_dim.8), calls=%async_computation.3 | async-start | bytes 262144 | tf_op jit(solution)/shard_map/all_to_all | solution.py:420
  193.8 1.6 broadcast.3.clone
  196.3 1.6 all-to-all-done.3
  198.7 1.9 constant_dynamic-update-slice_fusion.2
  200.6 1.9 constant_dynamic-update-slice_fusion.1
  202.5 8.6 %collective-permute-done.11 = bf16[2,32,32,128]{3,2,1,0:T(8,128)(2,1)S(1)} collective-permute-done((bf16[2,32,32,128]{3,2,1,0:T(8,128)(2,1)S(1)}, bf16[2,32,32,128]{3,2,1,0:T(8,128)(2,1)S(1)}, u32[]{:S(2)}, u32[]{:S(2)}) %collective-permute-start.11) | collective-permute-done | bytes 524320 | tf_op jit(solution)/shard_map/ppermute | solution.py:406
  212.9 29.6 %collective-permute-done.7 = bf16[2,32,32,128]{3,2,1,0:T(8,128)(2,1)S(1)} collective-permute-done((bf16[2,32,32,128]{3,2,1,0:T(8,128)(2,1)}, bf16[2,32,32,128]{3,2,1,0:T(8,128)(2,1)S(1)}, u32[]{:S(2)}, u32[]{:S(2)}) %collective-permute-start.7) | collective-permute-done | bytes 524320 | tf_op jit(solution)/shard_map/ppermute | solution.py:406
  243.3 10.7 %collective-permute-done.8 = bf16[2,32,32,128]{3,2,1,0:T(8,128)(2,1)S(1)} collective-permute-done((bf16[2,32,32,128]{3,2,1,0:T(8,128)(2,1)S(1)}, bf16[2,32,32,128]{3,2,1,0:T(8,128)(2,1)S(1)}, u32[]{:S(2)}, u32[]{:S(2)}) %collective-permute-start.8) | collective-permute-done | bytes 524320 | tf_op jit(solution)/shard_map/ppermute | solution.py:406
  (83 shorter events, 16.5 us)
Async XLA Ops:
  0.6 6.2 %copy-start.3 = (bf16[2,128,32,128]{3,2,1,0:T(8,128)(2,1)S(1)}, bf16[2,128,32,128]{3,2,1,0:T(8,128)(2,1)}, u32[]{:S(2)}) copy-start(bf16[2,128,32,128]{3,2,1,0:T(8,128)(2,1)} %own_ref.3) | copy-start | bytes 6291460
  3.3 8.2 %copy-start.21 = (f32[2,128,128]{2,1,0:T(8,128)S(1)}, f32[2,128,128]{2,1,0:T(8,128)}, u32[]{:S(2)}) copy-start(f32[2,128,128]{2,1,0:T(8,128)} %param.10) | copy-start | bytes 393220
  3.4 8.2 %copy-start.22 = (f32[128,128]{1,0:T(8,128)S(1)}, f32[128,128]{1,0:T(8,128)}, u32[]{:S(2)}) copy-start(f32[128,128]{1,0:T(8,128)} %param.11) | copy-start | bytes 196612
  3.4 23.6 %collective-permute-start = (bf16[2,32,32,128]{3,2,1,0:T(8,128)(2,1)}, bf16[2,32,32,128]{3,2,1,0:T(8,128)(2,1)}, u32[]{:S(2)}, u32[]{:S(2)}) collective-permute-start(bf16[2,32,32,128]{3,2,1,0:T(8,128)(2,1)} %get-tuple-element.88), channel_id=1, source_target_pairs={{0,1},{1,0},{2,3},{3,2},{4,5},{5,4},{6,7},{7,6},{8,9},{9,8},{10,11... | collective-permute-start | bytes 1572872 | tf_op jit(solution)/shard_map/ppermute | solution.py:406
  3.8 37.7 %collective-permute-start.1 = (bf16[2,32,32,128]{3,2,1,0:T(8,128)(2,1)}, bf16[2,32,32,128]{3,2,1,0:T(8,128)(2,1)}, u32[]{:S(2)}, u32[]{:S(2)}) collective-permute-start(bf16[2,32,32,128]{3,2,1,0:T(8,128)(2,1)} %get-tuple-element.87), channel_id=1, source_target_pairs={{0,2},{1,3},{2,0},{3,1},{4,6},{5,7},{6,4},{7,5},{8,10},{9,11},{10,... | collective-permute-start | bytes 1572872 | tf_op jit(solution)/shard_map/ppermute | solution.py:406
  6.4 69.8 %collective-permute-start.2 = (bf16[2,32,32,128]{3,2,1,0:T(8,128)(2,1)}, bf16[2,32,32,128]{3,2,1,0:T(8,128)(2,1)}, u32[]{:S(2)}, u32[]{:S(2)}) collective-permute-start(bf16[2,32,32,128]{3,2,1,0:T(8,128)(2,1)} %get-tuple-element.86), channel_id=1, source_target_pairs={{0,3},{1,2},{2,1},{3,0},{4,7},{5,6},{6,5},{7,4},{8,11},{9,10},{10,... | collective-permute-start | bytes 1572872 | tf_op jit(solution)/shard_map/ppermute | solution.py:406
  8.0 83.1 %collective-permute-start.3 = (bf16[2,32,32,128]{3,2,1,0:T(8,128)(2,1)}, bf16[2,32,32,128]{3,2,1,0:T(8,128)(2,1)S(1)}, u32[]{:S(2)}, u32[]{:S(2)}) collective-permute-start(bf16[2,32,32,128]{3,2,1,0:T(8,128)(2,1)} %get-tuple-element.85), channel_id=1, source_target_pairs={{0,1},{1,0},{2,3},{3,2},{4,5},{5,4},{6,7},{7,6},{8,9},{9,8},{10,11... | collective-permute-start | bytes 1572872 | tf_op jit(solution)/shard_map/ppermute | solution.py:406
  9.4 81.8 %collective-permute-start.4 = (bf16[2,32,32,128]{3,2,1,0:T(8,128)(2,1)}, bf16[2,32,32,128]{3,2,1,0:T(8,128)(2,1)S(1)}, u32[]{:S(2)}, u32[]{:S(2)}) collective-permute-start(bf16[2,32,32,128]{3,2,1,0:T(8,128)(2,1)} %get-tuple-element.84), channel_id=1, source_target_pairs={{0,2},{1,3},{2,0},{3,1},{4,6},{5,7},{6,4},{7,5},{8,10},{9,11},{10,... | collective-permute-start | bytes 1572872 | tf_op jit(solution)/shard_map/ppermute | solution.py:406
  11.7 4.4 %copy-start.9 = (f32[128,128]{1,0:T(8,128)}, f32[128,128]{1,0:T(8,128)S(1)}, u32[]{:S(2)}) copy-start(f32[128,128]{1,0:T(8,128)S(1)} %fusion.14.ham_ref) | copy-start | bytes 196612
  16.1 17.9 %copy-start.18 = (bf16[256,256]{1,0:T(8,128)(2,1)}, bf16[256,256]{1,0:T(8,128)(2,1)S(1)}, u32[]{:S(2)}) copy-start(bf16[256,256]{1,0:T(8,128)(2,1)S(1)} %get-tuple-element.45.low_ref) | copy-start | bytes 393220
  26.9 70.3 %collective-permute-start.5 = (bf16[2,32,32,128]{3,2,1,0:T(8,128)(2,1)}, bf16[2,32,32,128]{3,2,1,0:T(8,128)(2,1)}, u32[]{:S(2)}, u32[]{:S(2)}) collective-permute-start(bf16[2,32,32,128]{3,2,1,0:T(8,128)(2,1)} %get-tuple-element.83), channel_id=1, source_target_pairs={{0,3},{1,2},{2,1},{3,0},{4,7},{5,6},{6,5},{7,4},{8,11},{9,10},{10,... | collective-permute-start | bytes 1572872 | tf_op jit(solution)/shard_map/ppermute | solution.py:406
  29.9 4.1 %copy-start.20 = (bf16[2,128,32,128]{3,2,1,0:T(8,128)(2,1)S(1)}, bf16[2,128,32,128]{3,2,1,0:T(8,128)(2,1)}, u32[]{:S(2)}) copy-start(bf16[2,128,32,128]{3,2,1,0:T(8,128)(2,1)} %param.8) | copy-start | bytes 6291460
  34.9 62.3 %copy-start = (bf16[32,8,32,128]{3,1,2,0:T(8,128)(2,1)}, bf16[32,8,32,128]{3,1,2,0:T(8,128)(2,1)S(1)}, u32[]{:S(2)}) copy-start(bf16[32,8,32,128]{3,1,2,0:T(8,128)(2,1)S(1)} %copy.18) | copy-start | bytes 6291460
  76.1 1.6 copy-start.1
  77.7 1.6 copy-start.2
  97.3 1.6 copy-start.4
  103.3 0.6 copy-start.13
  104.0 12.8 %all-to-all-start = ((f32[32,1,128]{2,1,0:T(1,128)}), f32[32,1,128]{2,1,0:T(1,128)S(1)}, u32[]{:S(2)}, u32[]{:S(2)}) async-start(f32[32,1,128]{2,1,0:T(1,128)} %get-tuple-element.54), calls=%async_computation | async-start | bytes 32768 | tf_op jit(solution)/shard_map/all_to_all | solution.py:478
  109.0 7.8 %copy-start.10 = (f32[128,128]{1,0:T(8,128)S(1)}, f32[128,128]{1,0:T(8,128)}, u32[]{:S(2)}) copy-start(f32[128,128]{1,0:T(8,128)} %copy-done.9) | copy-start | bytes 196612
  109.0 7.8 %copy-start.14 = (f32[2,128,128]{2,1,0:T(8,128)S(1)}, f32[2,128,128]{2,1,0:T(8,128)}, u32[]{:S(2)}) copy-start(f32[2,128,128]{2,1,0:T(8,128)} %copy-done.13) | copy-start | bytes 393220
  116.8 0.9 copy-start.15
  123.2 0.7 copy-start.19
  123.8 21.3 %all-to-all-start.1 = ((f32[32,1,128]{2,1,0:T(1,128)}), f32[32,1,128]{2,1,0:T(1,128)S(1)}, u32[]{:S(2)}, u32[]{:S(2)}) async-start(f32[32,1,128]{2,1,0:T(1,128)} %get-tuple-element.61), calls=%async_computation.1 | async-start | bytes 32768 | tf_op jit(solution)/shard_map/all_to_all | solution.py:482
  145.1 4.5 %copy-start.16 = (f32[2,128,128]{2,1,0:T(8,128)S(1)}, f32[2,128,128]{2,1,0:T(8,128)}, u32[]{:S(2)}) copy-start(f32[2,128,128]{2,1,0:T(8,128)} %get-tuple-element.58.refs_1_.later_ref) | copy-start | bytes 393220
  145.1 4.5 %copy-start.17 = (f32[2,128,128]{2,1,0:T(8,128)S(1)}, f32[2,128,128]{2,1,0:T(8,128)}, u32[]{:S(2)}) copy-start(f32[2,128,128]{2,1,0:T(8,128)} %get-tuple-element.70.last_ref) | copy-start | bytes 393220
  149.5 6.5 %copy-start.6 = (bf16[256,4096]{1,0:T(8,128)(2,1)S(1)}, bf16[256,4096]{1,0:T(8,128)(2,1)}, u32[]{:S(2)}) copy-start(bf16[256,4096]{1,0:T(8,128)(2,1)} %get-tuple-element.77.col_ref) | copy-start | bytes 6291460
  151.8 18.6 %all-to-all-start.2 = ((f32[8,32,128]{2,1,0:T(8,128)}), f32[8,32,128]{2,1,0:T(8,128)S(1)}, u32[]{:S(2)}, u32[]{:S(2)}) async-start(f32[8,32,128]{2,1,0:T(8,128)} %bitcast.10), calls=%async_computation.2 | async-start | bytes 262144 | tf_op jit(solution)/shard_map/all_to_all | solution.py:412
  156.0 5.6 %copy-start.8 = (bf16[256,4096]{1,0:T(8,128)(2,1)S(1)}, bf16[256,4096]{1,0:T(8,128)(2,1)}, u32[]{:S(2)}) copy-start(bf16[256,4096]{1,0:T(8,128)(2,1)} %get-tuple-element.76.row_ref) | copy-start | bytes 6291460
  158.6 39.3 %collective-permute-start.9 = (bf16[2,32,32,128]{3,2,1,0:T(8,128)(2,1)}, bf16[2,32,32,128]{3,2,1,0:T(8,128)(2,1)}, u32[]{:S(2)}, u32[]{:S(2)}) collective-permute-start(bf16[2,32,32,128]{3,2,1,0:T(8,128)(2,1)} %get-tuple-element.79), channel_id=1, source_target_pairs={{0,1},{1,0},{2,3},{3,2},{4,5},{5,4},{6,7},{7,6},{8,9},{9,8},{10,11... | collective-permute-start | bytes 1572872 | tf_op jit(solution)/shard_map/ppermute | solution.py:406
  159.2 41.4 %collective-permute-start.10 = (bf16[2,32,32,128]{3,2,1,0:T(8,128)(2,1)}, bf16[2,32,32,128]{3,2,1,0:T(8,128)(2,1)}, u32[]{:S(2)}, u32[]{:S(2)}) collective-permute-start(bf16[2,32,32,128]{3,2,1,0:T(8,128)(2,1)} %get-tuple-element.80), channel_id=1, source_target_pairs={{0,2},{1,3},{2,0},{3,1},{4,6},{5,7},{6,4},{7,5},{8,10},{9,11},{10,... | collective-permute-start | bytes 1572872 | tf_op jit(solution)/shard_map/ppermute | solution.py:406
  162.9 1.9 copy-start.7
  167.9 6.1 %copy-start.5 = (bf16[256,4096]{1,0:T(8,128)(2,1)S(1)}, bf16[256,4096]{1,0:T(8,128)(2,1)}, u32[]{:S(2)}) copy-start(bf16[256,4096]{1,0:T(8,128)(2,1)} %get-tuple-element.71.col_ref) | copy-start | bytes 6291460
  170.4 14.4 %collective-permute-start.12 = (f32[32,128]{1,0:T(8,128)S(1)}, f32[32,128]{1,0:T(8,128)S(1)}, u32[]{:S(2)}, u32[]{:S(2)}) collective-permute-start(f32[32,128]{1,0:T(8,128)S(1)} %reduce_sum.19), channel_id=1, source_target_pairs={{0,1},{1,0},{2,3},{3,2},{4,5},{5,4},{6,7},{7,6},{8,9},{9,8},{10,11... | collective-permute-start | bytes 49160 | tf_op jit(solution)/shard_map/ppermute | solution.py:406
  172.0 14.3 %collective-permute-start.13 = (f32[32,128]{1,0:T(8,128)S(1)}, f32[32,128]{1,0:T(8,128)S(1)}, u32[]{:S(2)}, u32[]{:S(2)}) collective-permute-start(f32[32,128]{1,0:T(8,128)S(1)} %reduce_sum.19), channel_id=1, source_target_pairs={{0,2},{1,3},{2,0},{3,1},{4,6},{5,7},{6,4},{7,5},{8,10},{9,11},{10,... | collective-permute-start | bytes 49160 | tf_op jit(solution)/shard_map/ppermute | solution.py:406
  172.5 15.6 %collective-permute-start.14 = (f32[32,128]{1,0:T(8,128)S(1)}, f32[32,128]{1,0:T(8,128)S(1)}, u32[]{:S(2)}, u32[]{:S(2)}) collective-permute-start(f32[32,128]{1,0:T(8,128)S(1)} %reduce_sum.19), channel_id=1, source_target_pairs={{0,3},{1,2},{2,1},{3,0},{4,7},{5,6},{6,5},{7,4},{8,11},{9,10},{10,... | collective-permute-start | bytes 49160 | tf_op jit(solution)/shard_map/ppermute | solution.py:406
  176.6 0.8 copy-start.11
  184.8 13.1 %copy-start.12 = (bf16[2,32,32,128]{3,2,1,0:T(8,128)(2,1)S(1)}, bf16[2,32,32,128]{3,2,1,0:T(8,128)(2,1)}, u32[]{:S(2)}) copy-start(bf16[2,32,32,128]{3,2,1,0:T(8,128)(2,1)} %copy-done.11) | copy-start | bytes 1572868
  184.8 26.3 %collective-permute-start.11 = (bf16[2,32,32,128]{3,2,1,0:T(8,128)(2,1)S(1)}, bf16[2,32,32,128]{3,2,1,0:T(8,128)(2,1)S(1)}, u32[]{:S(2)}, u32[]{:S(2)}) collective-permute-start(bf16[2,32,32,128]{3,2,1,0:T(8,128)(2,1)S(1)} %get-tuple-element.81), channel_id=1, source_target_pairs={{0,3},{1,2},{2,1},{3,0},{4,7},{5,6},{6,5},{7,4},{8,11},{9,10},{10,... | collective-permute-start | bytes 1572872 | tf_op jit(solution)/shard_map/ppermute | solution.py:406
  186.2 25.7 %collective-permute-start.6 = (bf16[2,32,32,128]{3,2,1,0:T(8,128)(2,1)}, bf16[2,32,32,128]{3,2,1,0:T(8,128)(2,1)S(1)}, u32[]{:S(2)}, u32[]{:S(2)}) collective-permute-start(bf16[2,32,32,128]{3,2,1,0:T(8,128)(2,1)} %get-tuple-element.73), channel_id=1, source_target_pairs={{0,1},{1,0},{2,3},{3,2},{4,5},{5,4},{6,7},{7,6},{8,9},{9,8},{10,11... | collective-permute-start | bytes 1572872 | tf_op jit(solution)/shard_map/ppermute | solution.py:406
  188.0 54.4 %collective-permute-start.7 = (bf16[2,32,32,128]{3,2,1,0:T(8,128)(2,1)}, bf16[2,32,32,128]{3,2,1,0:T(8,128)(2,1)S(1)}, u32[]{:S(2)}, u32[]{:S(2)}) collective-permute-start(bf16[2,32,32,128]{3,2,1,0:T(8,128)(2,1)} %get-tuple-element.74), channel_id=1, source_target_pairs={{0,2},{1,3},{2,0},{3,1},{4,6},{5,7},{6,4},{7,5},{8,10},{9,11},{10,... | collective-permute-start | bytes 1572872 | tf_op jit(solution)/shard_map/ppermute | solution.py:406
  189.6 8.2 %all-to-all-start.3 = ((f32[8,32,128]{2,1,0:T(8,128)}), f32[8,32,128]{2,1,0:T(8,128)S(1)}, u32[]{:S(2)}, u32[]{:S(2)}) async-start(f32[8,32,128]{2,1,0:T(8,128)} %broadcast_in_dim.8), calls=%async_computation.3 | async-start | bytes 262144 | tf_op jit(solution)/shard_map/all_to_all | solution.py:420
  197.9 56.2 %collective-permute-start.8 = (bf16[2,32,32,128]{3,2,1,0:T(8,128)(2,1)S(1)}, bf16[2,32,32,128]{3,2,1,0:T(8,128)(2,1)S(1)}, u32[]{:S(2)}, u32[]{:S(2)}) collective-permute-start(bf16[2,32,32,128]{3,2,1,0:T(8,128)(2,1)S(1)} %copy-done.12), channel_id=1, source_target_pairs={{0,3},{1,2},{2,1},{3,0},{4,7},{5,6},{6,5},{7,4},{8,11},{9,10},{10,... | collective-permute-start | bytes 1572872 | tf_op jit(solution)/shard_map/ppermute | solution.py:406

commit v2 on v1

--- a/solution.py
+++ b/solution.py
@@ -319,22 +319,56 @@
     each_group(row_ref.shape[1], width, lambda base, g: advance_into(row_out, low, row_ref, base, width))
 
 
+def ready_kernel(parts, me_ref, col_ref, own_ref, *refs):
+    pieces, (low_first_ref, low_ref, out_ref, place, moved) = refs[: parts - 1], refs[parts - 1 :]
+    _, mirrored, block, times = pieces[0].shape
+    size, width = place.shape[0] // 2, place.shape[1]
+    own_width = col_ref.shape[1]
+    each_group(own_width, width, lambda base, g: advance_into(out_ref, low_ref[...], col_ref, base, width))
+    far = lax.bitwise_xor(me_ref[0], parts // 2) * (size // parts)
+    for r in range(parts):
+        source = lax.bitwise_xor(me_ref[0], r) * block
+        for part in range(2):
+            rows = pl.ds(pl.multiple_of(part * size + source, block), block)
+            for k in range(mirrored):
+                value = own_ref[part, far + k] if r == 0 else pieces[r - 1][part, k]
+                place[rows, pl.ds(k * times, times)] = value.astype(place.dtype)
+    span = min(SPAN, width)
+    for first in range(0, width, span):
+        lanes = pl.ds(first, span)
+        once = jnp.dot(low_first_ref[...], place[:, lanes].astype(jnp.bfloat16), preferred_element_type=jnp.float32)
+        moved[:, lanes] = once.astype(moved.dtype)
+        twice = jnp.dot(low_ref[...], moved[:, lanes], preferred_element_type=jnp.float32)
+        out_ref[:, pl.ds(own_width + first, span)] = twice.astype(out_ref.dtype)
+
+
 def last_kernel(parts, me_ref, col_ref, low_ref, *refs):
     outs, moved = refs[:parts], refs[parts]
-    _, _, block, times = outs[0].shape
+    _, rows_near, block, times = outs[0].shape
     width = moved.shape[1]
     size = moved.shape[0] // 2
+    group = width // times
+    count = rows_near - group
     low = low_ref[...]
 
     def body(base, g):
         first = lax.div(base, times)
         advance_into(moved, low, col_ref, base, width, local=True)
-        for r in range(parts):
+
+        def cut(r, offset):
             target = lax.bitwise_xor(me_ref[0], r) * block
             for part in range(2):
                 rows = pl.ds(pl.multiple_of(part * size + target, block), block)
-                for k in range(width // times):
-                    outs[r][part, first + k] = moved[rows, pl.ds(k * times, times)].astype(outs[r].dtype)
+                for k in range(group):
+                    outs[r][part, first + (k - offset)] = moved[rows, pl.ds(k * times, times)].astype(outs[r].dtype)
+
+        for r in range(parts // 2):
+            cut(r, 0)
+
+        @pl.when((first >= group) & (first < count))
+        def _():
+            for r in range(parts // 2, parts):
+                cut(r, group)
 
     each_group(col_ref.shape[1], width, body)
 
@@ -386,14 +420,26 @@
     return call(body, [(row.shape, jnp.bfloat16)], (row, low), cost(2, 1))[0]
 
 
-def last_step(me, col, low, parts, count, times):
+def ready_step(me, col, own, pieces, low_first, low):
     double = col.shape[0]
+    _, mirrored, block, times = pieces[0].shape
+    width = mirrored * times
+    out = ((double, col.shape[1] + width), jnp.bfloat16)
+    scratch = [pltpu.VMEM((double, width), place_type(block)), pltpu.VMEM((double, width), jnp.bfloat16)]
+    body = functools.partial(ready_kernel, len(pieces) + 1)
+    return call(body, [out], (me, col, own, *pieces, low_first, low), cost(3, 1), scratch, 1)[0]
+
+
+def last_step(me, ready, low, parts, mirrored, times):
+    double = ready.shape[0]
     block = double // 2 // parts
-    width = min(GROUP, count) * times
-    outs = [((2, count, block, times), jnp.bfloat16)] * parts
-    scratch = [pltpu.VMEM((double, width), place_type(block))]
+    count = ready.shape[1] // times - mirrored
+    near = ((2, count + mirrored, block, times), jnp.bfloat16)
+    far = ((2, count - mirrored, block, times), jnp.bfloat16)
+    outs = [near] * (parts // 2) + [far] * (parts - parts // 2)
+    scratch = [pltpu.VMEM((double, mirrored * times), place_type(block))]
     body = functools.partial(last_kernel, parts)
-    return call(body, outs, (me, col, low), cost(2, 1), scratch, 1)
+    return call(body, outs, (me, ready, low), cost(2, 1), scratch, 1)
 
 
 def tree_sum(values):
@@ -415,7 +461,9 @@
 
 def whole_total(share, shape):
     count = lax.axis_size("hist")
-    moved = [share] + [swap(share, "col", r) for r in range(1, lax.axis_size("col"))]
+    moved = [share]
+    for r in range(1, lax.axis_size("col")):
+        moved.append(swap(share, "col", r))
     share = tree_sum(moved)
     return lax.all_to_all(jnp.broadcast_to(share, (count,) + share.shape), "hist", 0, 0, tiled=True).reshape(shape)
 
@@ -444,13 +492,33 @@
     return pieces
 
 
+def mirror_slices(col, mirrored):
+    me, parts = lax.axis_index("col"), lax.axis_size("col")
+    count = col.shape[1] // parts
+    starts = [(me ^ r ^ (parts // 2)) * count for r in range(1, parts)]
+    return [lax.dynamic_slice_in_dim(col, start, mirrored, axis=1) for start in starts]
+
+
+def mirror_pieces(slices):
+    pieces = []
+    for r, piece in enumerate(slices, 1):
+        pieces.append(swap(piece, "col", r))
+    return pieces
+
+
 def return_pieces(pieces):
     me, parts = lax.axis_index("col"), lax.axis_size("col")
-    _, count, block, times = pieces[0].shape
+    _, near, block, times = pieces[0].shape
+    mirrored = (near - pieces[-1].shape[1]) // 2
+    count = near - mirrored
     out = jnp.zeros((2, parts * count, block, times), pieces[0].dtype)
     for r, piece in enumerate(pieces):
         moved = piece if r == 0 else swap(piece, "col", r)
-        out = lax.dynamic_update_slice_in_dim(out, moved, (me ^ r) * count, axis=1)
+        if r < parts // 2:
+            out = lax.dynamic_update_slice_in_dim(out, moved[:, :count], (me ^ r) * count, axis=1)
+            out = lax.dynamic_update_slice_in_dim(out, moved[:, count:], (me ^ r ^ (parts // 2)) * count, axis=1)
+        else:
+            out = lax.dynamic_update_slice_in_dim(out, moved, (me ^ r) * count + mirrored, axis=1)
     return out
 
 
@@ -460,41 +528,49 @@
     devices = parts * lax.axis_size("hist")
     me = lax.axis_index("col").astype(jnp.int32).reshape(1)
     width = min(GROUP, count) * times
+    mirrored = count // 4
 
     great_pieces = gather_pieces(great_col)
     less_pieces = gather_pieces(less_col)
+    great_slices = mirror_slices(great_col, mirrored)
+    less_slices = mirror_slices(less_col, mirrored)
 
     symmetric = 0.5 * (hamiltonian + hamiltonian.T)
-    low, unit = solve(diagonal_row(density[0]).reshape(1, 1, size), symmetric)
+    low_first, unit = solve(diagonal_row(density[0]).reshape(1, 1, size), symmetric)
     known = rotate(unit, density * (1.0 / devices))
 
     less = less_row.reshape(2 * size, count * times)
     great = great_row.reshape(2 * size, count * times)
     cols_great, minus = now_step(me, less, great_col, great_pieces)
-    less, cols_great, minus_later = later_step(less, cols_great, low, width)
+    less, cols_great, minus_later = later_step(less, cols_great, low_first, width)
     less_pieces, minus_later = lax.optimization_barrier((less_pieces, minus_later))
+    great_slices, _ = lax.optimization_barrier((great_slices, less_pieces[0]))
+    great_far = mirror_pieces(great_slices)
     cols_less, rho, part = now_step(me, great, less_col, less_pieces, minus, known, devices)
 
     levels = lax.all_to_all(part, ("hist", "col"), 0, 0, tiled=True)
-    great, cols_less, later = later_step(great, cols_less, low, width, minus_later)
+    great, cols_less, later = later_step(great, cols_less, low_first, width, minus_later)
     low, unit, left, part = solve(levels, symmetric, rho, later)
 
     levels = lax.all_to_all(part, ("hist", "col"), 0, 0, tiled=True)
-    less, cols_great, minus = later_step(less, cols_great, low, width)
+    less_slices, _ = lax.optimization_barrier((less_slices, part))
+    less_far = mirror_pieces(less_slices)
+    great_ready = ready_step(me, cols_great, great_col, great_far, low_first, low)
     low_last, unit_last = solve(levels, symmetric)
 
-    great_out = return_pieces(last_step(me, cols_great, low_last, parts, count, times))
-    great, cols_less, last = later_step(great, cols_less, low, width, minus)
-    low = low_last
+    great_out = return_pieces(last_step(me, great_ready, low_last, parts, mirrored, times))
+    less, _, minus = later_step(less, cols_great, low, width)
+    great, _, last = later_step(great, cols_less, low, width, minus)
     args = (left, unit, later, unit_last, last)
     estimate = pl.CostEstimate(flops=500_000_000, bytes_accessed=1_000_000, transcendentals=0)
     rho = call(finish_kernel, [(density.shape, jnp.float32)], args, estimate)[0]
     share = part_total(rho)
-    cols_less, share = lax.optimization_barrier((cols_less, share))
-    less_out = return_pieces(last_step(me, cols_less, low, parts, count, times))
+    less_ready = ready_step(me, cols_less, less_col, less_far, low_first, low)
+    less_ready, share = lax.optimization_barrier((less_ready, share))
+    less_out = return_pieces(last_step(me, less_ready, low_last, parts, mirrored, times))
     rho = whole_total(share, density.shape)
-    less_row_out = row_step(less, low, width).reshape(less_row.shape)
-    great_row_out = row_step(great, low, width).reshape(great_row.shape)
+    less_row_out = row_step(less, low_last, width).reshape(less_row.shape)
+    great_row_out = row_step(great, low_last, width).reshape(great_row.shape)
     return (less_row_out, less_out, great_row_out, great_out, rho)
 
 

time: 256 us -> 264 us (1.031)
  the two profiles are of different devices: /device:TPU:10 before, /device:TPU:0 now
where the time goes in v2:
time: 264 us; the launch traced here: 259 us
  waiting for transfers between devices  79.1 us (30%)
  Pallas kernels  67.5 us (26%)
  starting transfers between devices  63.9 us (24%)
  local copies, waits for them, and re-layouts  45.2 us (17%)
    ppermute x21, waiting for transfers between devices, swap(): lax.ppermute(value, name, [(j, j ^ r) for j in range(lax.axis_size(name))])  75.1 us
    pallas_call x16, Pallas kernels, call(): pl.pallas_call(body, out_shape=[pltpu.HBM(shape, kind) if i in streamed_o...  67.5 us
    ppermute x21, starting transfers between devices, swap(): lax.ppermute(value, name, [(j, j ^ r) for j in range(lax.axis_size(name))])  36.5 us
    unnamed x74, local copies, waits for them, and re-layouts  21.5 us
    all_to_all x2, starting transfers between devices, per_device(): levels = lax.all_to_all(part, ('hist', 'col'), 0, 0, tiled=True)  19.9 us
  transfers between devices with their start and end apart: 25, of which 7 were waited for; matrix products, arithmetic and copies ran while one was open for 12% of the time, Pallas kernels for 24%

profile of v2, /device:TPU:0, one launch (start us, length us, event | category | flops | bytes accessed | tf_op | source)
XLA Modules:
  0.0 258.8 jit_solution(2716114341951744902)
XLA Ops:
  0.7 2.7 %constant_dynamic-slice_fusion.9 = (bf16[2,32,32,128]{3,2,1,0:T(8,128)(2,1)}, bf16[2,32,32,128]{3,2,1,0:T(8,128)(2,1)}, bf16[2,32,32,128]{3,2,1,0:T(8,128)(2,1)}) fusion(bf16[2,128,32,128]{3,2,1,0:T(8,128)(2,1)} %own_ref.7, s32[]{:T(128)S(6)} %select_n.24, s32[]{:T(128)S(6)} %select_n.23, s32[]{:T(128)S(6)} %select_n.22), kind=kLoop, calls=%fused_computation.59 | loop fusion | bytes 3145740 | tf_op jit(solution)/shard_map/dynamic_slice | solution.py:490
  3.4 3.1 %collective-permute-start = (bf16[2,32,32,128]{3,2,1,0:T(8,128)(2,1)}, bf16[2,32,32,128]{3,2,1,0:T(8,128)(2,1)}, u32[]{:S(2)}, u32[]{:S(2)}) collective-permute-start(bf16[2,32,32,128]{3,2,1,0:T(8,128)(2,1)} %get-tuple-element.102), channel_id=1, source_target_pairs={{0,1},{1,0},{2,3},{3,2},{4,5},{5,4},{6,7},{7,6},{8,9},{9,8},{10,11... | collective-permute-start | bytes 1572872 | tf_op jit(solution)/shard_map/ppermute | solution.py:452
  6.4 2.6 %collective-permute-start.1 = (bf16[2,32,32,128]{3,2,1,0:T(8,128)(2,1)}, bf16[2,32,32,128]{3,2,1,0:T(8,128)(2,1)}, u32[]{:S(2)}, u32[]{:S(2)}) collective-permute-start(bf16[2,32,32,128]{3,2,1,0:T(8,128)(2,1)} %get-tuple-element.101), channel_id=1, source_target_pairs={{0,2},{1,3},{2,0},{3,1},{4,6},{5,7},{6,4},{7,5},{8,10},{9,11},{10,... | collective-permute-start | bytes 1572872 | tf_op jit(solution)/shard_map/ppermute | solution.py:452
  11.1 3.5 %collective-permute-start.4 = (bf16[2,32,32,128]{3,2,1,0:T(8,128)(2,1)}, bf16[2,32,32,128]{3,2,1,0:T(8,128)(2,1)S(1)}, u32[]{:S(2)}, u32[]{:S(2)}) collective-permute-start(bf16[2,32,32,128]{3,2,1,0:T(8,128)(2,1)} %get-tuple-element.98), channel_id=1, source_target_pairs={{0,2},{1,3},{2,0},{3,1},{4,6},{5,7},{6,4},{7,5},{8,10},{9,11},{10,... | collective-permute-start | bytes 1572872 | tf_op jit(solution)/shard_map/ppermute | solution.py:452
  14.8 4.4 %shard_map.102 = (bf16[256,256]{1,0:T(8,128)(2,1)S(1)}, f32[2,128,128]{2,1,0:T(8,128)S(1)}) custom-call(f32[1,1,128]{2,1,0:T(1,128)S(1)} %bitcast.68, f32[128,128]{1,0:T(8,128)S(1)} %fusion.14.ham_ref), custom_call_target="tpu_custom_call" | custom-call | flops 4000000000 | bytes 1000000 | tf_op jit(solution)/shard_map/pallas_call | solution.py:117
  21.8 8.2 %collective-permute-done.refs_0_ = bf16[2,32,32,128]{3,2,1,0:T(8,128)(2,1)} collective-permute-done((bf16[2,32,32,128]{3,2,1,0:T(8,128)(2,1)}, bf16[2,32,32,128]{3,2,1,0:T(8,128)(2,1)}, u32[]{:S(2)}, u32[]{:S(2)}) %collective-permute-start) | collective-permute-done | bytes 524320 | tf_op jit(solution)/shard_map/ppermute | solution.py:452
  30.0 4.5 %collective-permute-start.5 = (bf16[2,32,32,128]{3,2,1,0:T(8,128)(2,1)}, bf16[2,32,32,128]{3,2,1,0:T(8,128)(2,1)}, u32[]{:S(2)}, u32[]{:S(2)}) collective-permute-start(bf16[2,32,32,128]{3,2,1,0:T(8,128)(2,1)} %get-tuple-element.97), channel_id=1, source_target_pairs={{0,3},{1,2},{2,1},{3,0},{4,7},{5,6},{6,5},{7,4},{8,11},{9,10},{10,... | collective-permute-start | bytes 1572872 | tf_op jit(solution)/shard_map/ppermute | solution.py:452
  34.6 2.3 copy.19
  36.9 2.3 copy.18
  39.2 1.8 constant_dynamic-slice_fusion.3
  41.8 3.1 %collective-permute-done.1.refs_1_ = bf16[2,32,32,128]{3,2,1,0:T(8,128)(2,1)} collective-permute-done((bf16[2,32,32,128]{3,2,1,0:T(8,128)(2,1)}, bf16[2,32,32,128]{3,2,1,0:T(8,128)(2,1)}, u32[]{:S(2)}, u32[]{:S(2)}) %collective-permute-start.1) | collective-permute-done | bytes 524320 | tf_op jit(solution)/shard_map/ppermute | solution.py:452
  44.9 1.6 copy-done.5
  46.5 4.2 %shard_map.101 = (bf16[256,4096]{1,0:T(8,128)(2,1)}, f32[256,256]{1,0:T(8,128)S(1)}) custom-call(s32[1]{0:T(128)} %bitcast.me_ref, bf16[256,4096]{1,0:T(8,128)(2,1)S(1)} %bitcast.65, bf16[2,128,32,128]{3,2,1,0:T(8,128)(2,1)S(1)} %copy-done, bf16[2,32,32,128]{3,2,1,0:T(8,128)(2,1)} %collective-permute-done.refs_0_, ...), custom_call_target="tpu_custom_call" | custom-call | flops 1073741824 | bytes 8388608 | tf_op jit(solution)/shard_map/pallas_call | solution.py:117
  50.7 7.7 %shard_map.103 = (bf16[256,4096]{1,0:T(8,128)(2,1)}, bf16[256,4096]{1,0:T(8,128)(2,1)}, f32[256,256]{1,0:T(8,128)}) custom-call(bf16[256,4096]{1,0:T(8,128)(2,1)} %bitcast.64, bf16[256,4096]{1,0:T(8,128)(2,1)} %get-tuple-element.48.col_hbm, bf16[256,256]{1,0:T(8,128)(2,1)} %copy-done.10), custom_call_target="tpu_custom_call" | custom-call | flops 1610612736 | bytes 8388608 | tf_op jit(solution)/shard_map/pallas_call | solution.py:117
  58.4 31.4 %collective-permute-done.4.refs_1_ = bf16[2,32,32,128]{3,2,1,0:T(8,128)(2,1)S(1)} collective-permute-done((bf16[2,32,32,128]{3,2,1,0:T(8,128)(2,1)}, bf16[2,32,32,128]{3,2,1,0:T(8,128)(2,1)S(1)}, u32[]{:S(2)}, u32[]{:S(2)}) %collective-permute-start.4) | collective-permute-done | bytes 524320 | tf_op jit(solution)/shard_map/ppermute | solution.py:452
  89.8 1.6 copy-done.2
  93.0 4.5 %shard_map.104 = (bf16[256,4096]{1,0:T(8,128)(2,1)}, f32[2,128,128]{2,1,0:T(8,128)S(1)}, f32[32,1,128]{2,1,0:T(1,128)}) custom-call(s32[1]{0:T(128)} %bitcast.me_ref, bf16[256,4096]{1,0:T(8,128)(2,1)S(1)} %bitcast.63, bf16[2,128,32,128]{3,2,1,0:T(8,128)(2,1)S(1)} %copy-done.2, bf16[2,32,32,128]{3,2,1,0:T(8,128)(2,1)S(1)} %collective-permute-done.3.refs_0_, ...), custom_call_target="tpu_custom_call" | custom-call | flops 1073741824 | bytes 8388608 | tf_op jit(solution)/shard_map/pallas_call | solution.py:117
  98.1 14.0 %all-to-all-start = ((f32[32,1,128]{2,1,0:T(1,128)}), f32[32,1,128]{2,1,0:T(1,128)S(1)}, u32[]{:S(2)}, u32[]{:S(2)}) async-start(f32[32,1,128]{2,1,0:T(1,128)} %get-tuple-element.58), calls=%async_computation | async-start | bytes 32768 | tf_op jit(solution)/shard_map/all_to_all | solution.py:551
  112.1 1.7 collective-permute-start.12
  113.7 2.4 collective-permute-start.13
  116.5 7.8 %shard_map.105 = (bf16[256,4096]{1,0:T(8,128)(2,1)}, bf16[256,4096]{1,0:T(8,128)(2,1)}, f32[2,128,128]{2,1,0:T(8,128)}) custom-call(bf16[256,4096]{1,0:T(8,128)(2,1)} %bitcast.62, bf16[256,4096]{1,0:T(8,128)(2,1)} %get-tuple-element.60.col_hbm, bf16[256,256]{1,0:T(8,128)(2,1)} %copy-done.10, f32[256,256]{1,0:T(8,128)} %get-tuple-element.61.refs_0_), custom_call_target="tpu_custom_call" | custom-call | flops 1610612736 | bytes 8388608 | tf_op jit(solution)/shard_map/pallas_call | solution.py:117
  125.3 5.4 %shard_map.106 = (bf16[256,256]{1,0:T(8,128)(2,1)S(1)}, f32[2,128,128]{2,1,0:T(8,128)S(1)}, f32[2,128,128]{2,1,0:T(8,128)S(1)}, f32[32,1,128]{2,1,0:T(1,128)}) custom-call(f32[32,1,128]{2,1,0:T(1,128)S(1)} %all-to-all-done.levels_ref, f32[128,128]{1,0:T(8,128)S(1)} %copy-done.15, f32[2,128,128]{2,1,0:T(8,128)S(1)} %copy-done.25, f32[2,128,128]{2,1,0:T(8,128)S(1)} %copy-done.26), custom_call_target="tpu_custom_call" | custom-call | flops 4000000000 | bytes 1000000 | tf_op jit(solution)/shard_map/pallas_call | solution.py:117
  131.4 5.9 %all-to-all-start.1 = ((f32[32,1,128]{2,1,0:T(1,128)}), f32[32,1,128]{2,1,0:T(1,128)S(1)}, u32[]{:S(2)}, u32[]{:S(2)}) async-start(f32[32,1,128]{2,1,0:T(1,128)} %get-tuple-element.65), calls=%async_computation.1 | async-start | bytes 32768 | tf_op jit(solution)/shard_map/all_to_all | solution.py:555
  137.2 1.6 collective-permute-start.6
  138.9 2.4 collective-permute-start.7
  141.3 7.7 %shard_map.107 = (bf16[256,4096]{1,0:T(8,128)(2,1)}, bf16[256,4096]{1,0:T(8,128)(2,1)}, f32[256,256]{1,0:T(8,128)}) custom-call(bf16[256,4096]{1,0:T(8,128)(2,1)} %get-tuple-element.50.row_hbm, bf16[256,4096]{1,0:T(8,128)(2,1)} %get-tuple-element.51.col_hbm.col_ref, bf16[256,256]{1,0:T(8,128)(2,1)} %copy-done.12), custom_call_target="tpu_custom_call" | custom-call | flops 1610612736 | bytes 8388608 | tf_op jit(solution)/shard_map/pallas_call | solution.py:117
  148.9 7.7 %shard_map.111 = (bf16[256,4096]{1,0:T(8,128)(2,1)}, bf16[256,4096]{1,0:T(8,128)(2,1)}, f32[2,128,128]{2,1,0:T(8,128)}) custom-call(bf16[256,4096]{1,0:T(8,128)(2,1)} %get-tuple-element.74.row_hbm, bf16[256,4096]{1,0:T(8,128)(2,1)} %get-tuple-element.67.col_ref.col_hbm, bf16[256,256]{1,0:T(8,128)(2,1)} %copy-done.12, f32[256,256]{1,0:T(8,128)} %get-tuple-element.75.refs_0_), custom_call_target="tpu_custom_call" | custom-call | flops 1610612736 | bytes 8388608 | tf_op jit(solution)/shard_map/pallas_call | solution.py:117
  156.7 4.4 %shard_map.108 = (bf16[256,256]{1,0:T(8,128)(2,1)S(1)}, f32[2,128,128]{2,1,0:T(8,128)S(1)}) custom-call(f32[32,1,128]{2,1,0:T(1,128)S(1)} %all-to-all-done.1.levels_ref, f32[128,128]{1,0:T(8,128)S(1)} %copy-done.15), custom_call_target="tpu_custom_call" | custom-call | flops 4000000000 | bytes 1000000 | tf_op jit(solution)/shard_map/pallas_call | solution.py:117
  161.1 2.3 shard_map.112
  163.4 3.7 %all-to-all-start.2 = ((f32[8,32,128]{2,1,0:T(8,128)}), f32[8,32,128]{2,1,0:T(8,128)S(1)}, u32[]{:S(2)}, u32[]{:S(2)}) async-start(f32[8,32,128]{2,1,0:T(8,128)} %bitcast.10), calls=%async_computation.2 | async-start | bytes 262144 | tf_op jit(solution)/shard_map/all_to_all | solution.py:458
  170.0 1.8 copy.15
  173.2 1.8 copy.14
  175.5 2.0 shard_map.115.col_ref
  177.6 2.9 %shard_map.116 = (bf16[2,40,32,128]{3,2,1,0:T(8,128)(2,1)S(1)}, bf16[2,40,32,128]{3,2,1,0:T(8,128)(2,1)}, bf16[2,24,32,128]{3,2,1,0:T(8,128)(2,1)}, bf16[2,24,32,128]{3,2,1,0:T(8,128)(2,1)S(1)}) custom-call(s32[1]{0:T(128)} %bitcast.me_ref, bf16[256,5120]{1,0:T(8,128)(2,1)S(1)} %shard_map.115.col_ref, bf16[256,256]{1,0:T(8,128)(2,1)S(1)} %get-tuple-element.66.low_ref), custom_call_target="tpu_custom_call" | custom-call | flops 536870912 | bytes 4194304 | tf_op jit(solution)/shard_map/pallas_call | solution.py:117
  185.0 3.4 %collective-permute-start.16 = (bf16[2,24,32,128]{3,2,1,0:T(8,128)(2,1)}, bf16[2,24,32,128]{3,2,1,0:T(8,128)(2,1)}, u32[]{:S(2)}, u32[]{:S(2)}) collective-permute-start(bf16[2,24,32,128]{3,2,1,0:T(8,128)(2,1)} %get-tuple-element.88), channel_id=1, source_target_pairs={{0,2},{1,3},{2,0},{3,1},{4,6},{5,7},{6,4},{7,5},{8,10},{9,11},{10,... | collective-permute-start | bytes 1179656 | tf_op jit(solution)/shard_map/ppermute | solution.py:452
  188.3 2.0 shard_map.110.col_ref
  191.5 3.4 %collective-permute-start.20 = (f32[32,128]{1,0:T(8,128)S(1)}, f32[32,128]{1,0:T(8,128)S(1)}, u32[]{:S(2)}, u32[]{:S(2)}) collective-permute-start(f32[32,128]{1,0:T(8,128)S(1)} %reduce_sum.19), channel_id=1, source_target_pairs={{0,3},{1,2},{2,1},{3,0},{4,7},{5,6},{6,5},{7,4},{8,11},{9,10},{10,... | collective-permute-start | bytes 49160 | tf_op jit(solution)/shard_map/ppermute | solution.py:452
  194.8 1.9 shard_map.113
  199.2 1.6 broadcast.3.clone
  201.7 9.1 %collective-permute-done.18 = f32[32,128]{1,0:T(8,128)S(1)} collective-permute-done((f32[32,128]{1,0:T(8,128)S(1)}, f32[32,128]{1,0:T(8,128)S(1)}, u32[]{:S(2)}, u32[]{:S(2)}) %collective-permute-start.18) | collective-permute-done | bytes 16416 | tf_op jit(solution)/shard_map/ppermute | solution.py:452
  210.7 3.6 %collective-permute-start.17 = (bf16[2,24,32,128]{3,2,1,0:T(8,128)(2,1)S(1)}, bf16[2,24,32,128]{3,2,1,0:T(8,128)(2,1)}, u32[]{:S(2)}, u32[]{:S(2)}) collective-permute-start(bf16[2,24,32,128]{3,2,1,0:T(8,128)(2,1)S(1)} %copy-done.19), channel_id=1, source_target_pairs={{0,3},{1,2},{2,1},{3,0},{4,7},{5,6},{6,5},{7,4},{8,11},{9,10},{10,... | collective-permute-start | bytes 1179656 | tf_op jit(solution)/shard_map/ppermute | solution.py:452
  215.0 3.8 %all-to-all-start.3 = ((f32[8,32,128]{2,1,0:T(8,128)}), f32[8,32,128]{2,1,0:T(8,128)S(1)}, u32[]{:S(2)}, u32[]{:S(2)}) async-start(f32[8,32,128]{2,1,0:T(8,128)} %broadcast_in_dim.8), calls=%async_computation.3 | async-start | bytes 262144 | tf_op jit(solution)/shard_map/all_to_all | solution.py:468
  220.3 4.0 %all-to-all-done.3 = f32[8,32,128]{2,1,0:T(8,128)S(1)} async-done(((f32[8,32,128]{2,1,0:T(8,128)}), f32[8,32,128]{2,1,0:T(8,128)S(1)}, u32[]{:S(2)}, u32[]{:S(2)}) %all-to-all-start.3) | async-done | bytes 131104 | tf_op jit(solution)/shard_map/all_to_all | solution.py:468
  224.5 1.9 slice_dynamic-update-slice_fusion
  228.1 1.8 constant_dynamic-update-slice_fusion.1
  229.9 1.8 constant_dynamic-update-slice_fusion
  231.7 13.6 %collective-permute-done.9 = bf16[2,40,32,128]{3,2,1,0:T(8,128)(2,1)S(1)} collective-permute-done((bf16[2,40,32,128]{3,2,1,0:T(8,128)(2,1)S(1)}, bf16[2,40,32,128]{3,2,1,0:T(8,128)(2,1)S(1)}, u32[]{:S(2)}, u32[]{:S(2)}) %collective-permute-start.9) | collective-permute-done | bytes 655392 | tf_op jit(solution)/shard_map/ppermute | solution.py:452
  246.8 9.7 %collective-permute-done.10 = bf16[2,24,32,128]{3,2,1,0:T(8,128)(2,1)S(1)} collective-permute-done((bf16[2,24,32,128]{3,2,1,0:T(8,128)(2,1)S(1)}, bf16[2,24,32,128]{3,2,1,0:T(8,128)(2,1)S(1)}, u32[]{:S(2)}, u32[]{:S(2)}) %collective-permute-start.10) | collective-permute-done | bytes 393248 | tf_op jit(solution)/shard_map/ppermute | solution.py:452
  (125 shorter events, 31.3 us)
Async XLA Ops:
  0.6 8.4 %copy-start.1 = (bf16[2,128,32,128]{3,2,1,0:T(8,128)(2,1)S(1)}, bf16[2,128,32,128]{3,2,1,0:T(8,128)(2,1)}, u32[]{:S(2)}) copy-start(bf16[2,128,32,128]{3,2,1,0:T(8,128)(2,1)} %own_ref.6) | copy-start | bytes 6291460
  3.4 11.3 %copy-start.31 = (f32[2,128,128]{2,1,0:T(8,128)S(1)}, f32[2,128,128]{2,1,0:T(8,128)}, u32[]{:S(2)}) copy-start(f32[2,128,128]{2,1,0:T(8,128)} %param.10) | copy-start | bytes 393220
  3.4 11.3 %copy-start.32 = (f32[128,128]{1,0:T(8,128)S(1)}, f32[128,128]{1,0:T(8,128)}, u32[]{:S(2)}) copy-start(f32[128,128]{1,0:T(8,128)} %param.11) | copy-start | bytes 196612
  3.4 26.6 %collective-permute-start = (bf16[2,32,32,128]{3,2,1,0:T(8,128)(2,1)}, bf16[2,32,32,128]{3,2,1,0:T(8,128)(2,1)}, u32[]{:S(2)}, u32[]{:S(2)}) collective-permute-start(bf16[2,32,32,128]{3,2,1,0:T(8,128)(2,1)} %get-tuple-element.102), channel_id=1, source_target_pairs={{0,1},{1,0},{2,3},{3,2},{4,5},{5,4},{6,7},{7,6},{8,9},{9,8},{10,11... | collective-permute-start | bytes 1572872 | tf_op jit(solution)/shard_map/ppermute | solution.py:452
  6.4 38.5 %collective-permute-start.1 = (bf16[2,32,32,128]{3,2,1,0:T(8,128)(2,1)}, bf16[2,32,32,128]{3,2,1,0:T(8,128)(2,1)}, u32[]{:S(2)}, u32[]{:S(2)}) collective-permute-start(bf16[2,32,32,128]{3,2,1,0:T(8,128)(2,1)} %get-tuple-element.101), channel_id=1, source_target_pairs={{0,2},{1,3},{2,0},{3,1},{4,6},{5,7},{6,4},{7,5},{8,10},{9,11},{10,... | collective-permute-start | bytes 1572872 | tf_op jit(solution)/shard_map/ppermute | solution.py:452
  9.0 35.9 %collective-permute-start.2 = (bf16[2,32,32,128]{3,2,1,0:T(8,128)(2,1)}, bf16[2,32,32,128]{3,2,1,0:T(8,128)(2,1)}, u32[]{:S(2)}, u32[]{:S(2)}) collective-permute-start(bf16[2,32,32,128]{3,2,1,0:T(8,128)(2,1)} %get-tuple-element.100), channel_id=1, source_target_pairs={{0,3},{1,2},{2,1},{3,0},{4,7},{5,6},{6,5},{7,4},{8,11},{9,10},{10,... | collective-permute-start | bytes 1572872 | tf_op jit(solution)/shard_map/ppermute | solution.py:452
  10.2 48.2 %collective-permute-start.3 = (bf16[2,32,32,128]{3,2,1,0:T(8,128)(2,1)}, bf16[2,32,32,128]{3,2,1,0:T(8,128)(2,1)S(1)}, u32[]{:S(2)}, u32[]{:S(2)}) collective-permute-start(bf16[2,32,32,128]{3,2,1,0:T(8,128)(2,1)} %get-tuple-element.99), channel_id=1, source_target_pairs={{0,1},{1,0},{2,3},{3,2},{4,5},{5,4},{6,7},{7,6},{8,9},{9,8},{10,11... | collective-permute-start | bytes 1572872 | tf_op jit(solution)/shard_map/ppermute | solution.py:452
  11.1 78.6 %collective-permute-start.4 = (bf16[2,32,32,128]{3,2,1,0:T(8,128)(2,1)}, bf16[2,32,32,128]{3,2,1,0:T(8,128)(2,1)S(1)}, u32[]{:S(2)}, u32[]{:S(2)}) collective-permute-start(bf16[2,32,32,128]{3,2,1,0:T(8,128)(2,1)} %get-tuple-element.98), channel_id=1, source_target_pairs={{0,2},{1,3},{2,0},{3,1},{4,6},{5,7},{6,4},{7,5},{8,10},{9,11},{10,... | collective-permute-start | bytes 1572872 | tf_op jit(solution)/shard_map/ppermute | solution.py:452
  14.8 4.4 %copy-start.14 = (f32[128,128]{1,0:T(8,128)}, f32[128,128]{1,0:T(8,128)S(1)}, u32[]{:S(2)}) copy-start(f32[128,128]{1,0:T(8,128)S(1)} %fusion.14.ham_ref) | copy-start | bytes 196612
  19.8 14.7 %copy-start.29 = (bf16[2,128,32,128]{3,2,1,0:T(8,128)(2,1)S(1)}, bf16[2,128,32,128]{3,2,1,0:T(8,128)(2,1)}, u32[]{:S(2)}) copy-start(bf16[2,128,32,128]{3,2,1,0:T(8,128)(2,1)} %param.6) | copy-start | bytes 6291460
  30.0 59.8 %collective-permute-start.5 = (bf16[2,32,32,128]{3,2,1,0:T(8,128)(2,1)}, bf16[2,32,32,128]{3,2,1,0:T(8,128)(2,1)}, u32[]{:S(2)}, u32[]{:S(2)}) collective-permute-start(bf16[2,32,32,128]{3,2,1,0:T(8,128)(2,1)} %get-tuple-element.97), channel_id=1, source_target_pairs={{0,3},{1,2},{2,1},{3,0},{4,7},{5,6},{6,5},{7,4},{8,11},{9,10},{10,... | collective-permute-start | bytes 1572872 | tf_op jit(solution)/shard_map/ppermute | solution.py:452
  34.6 2.3 copy-start.30
  36.9 4.1 %copy-start = (bf16[2,128,32,128]{3,2,1,0:T(8,128)(2,1)S(1)}, bf16[2,128,32,128]{3,2,1,0:T(8,128)(2,1)}, u32[]{:S(2)}) copy-start(bf16[2,128,32,128]{3,2,1,0:T(8,128)(2,1)} %own_ref.7) | copy-start | bytes 6291460
  89.8 1.6 copy-start.2
  98.1 26.3 %all-to-all-start = ((f32[32,1,128]{2,1,0:T(1,128)}), f32[32,1,128]{2,1,0:T(1,128)S(1)}, u32[]{:S(2)}, u32[]{:S(2)}) async-start(f32[32,1,128]{2,1,0:T(1,128)} %get-tuple-element.58), calls=%async_computation | async-start | bytes 32768 | tf_op jit(solution)/shard_map/all_to_all | solution.py:551
  112.1 63.0 %collective-permute-start.12 = (bf16[2,8,32,128]{3,2,1,0:T(8,128)(2,1)}, bf16[2,8,32,128]{3,2,1,0:T(8,128)(2,1)S(1)}, u32[]{:S(2)}, u32[]{:S(2)}) collective-permute-start(bf16[2,8,32,128]{3,2,1,0:T(8,128)(2,1)} %get-tuple-element.83), channel_id=1, source_target_pairs={{0,1},{1,0},{2,3},{3,2},{4,5},{5,4},{6,7},{7,6},{8,9},{9,8},{10,11... | collective-permute-start | bytes 393224 | tf_op jit(solution)/shard_map/ppermute | solution.py:452
  113.7 61.8 %collective-permute-start.13 = (bf16[2,8,32,128]{3,2,1,0:T(8,128)(2,1)}, bf16[2,8,32,128]{3,2,1,0:T(8,128)(2,1)S(1)}, u32[]{:S(2)}, u32[]{:S(2)}) collective-permute-start(bf16[2,8,32,128]{3,2,1,0:T(8,128)(2,1)} %get-tuple-element.84), channel_id=1, source_target_pairs={{0,2},{1,3},{2,0},{3,1},{4,6},{5,7},{6,4},{7,5},{8,10},{9,11},{10,... | collective-permute-start | bytes 393224 | tf_op jit(solution)/shard_map/ppermute | solution.py:452
  116.1 59.4 %collective-permute-start.14 = (bf16[2,8,32,128]{3,2,1,0:T(8,128)(2,1)}, bf16[2,8,32,128]{3,2,1,0:T(8,128)(2,1)S(1)}, u32[]{:S(2)}, u32[]{:S(2)}) collective-permute-start(bf16[2,8,32,128]{3,2,1,0:T(8,128)(2,1)} %get-tuple-element.85), channel_id=1, source_target_pairs={{0,3},{1,2},{2,1},{3,0},{4,7},{5,6},{6,5},{7,4},{8,11},{9,10},{10,... | collective-permute-start | bytes 393224 | tf_op jit(solution)/shard_map/ppermute | solution.py:452
  116.5 7.8 %copy-start.15 = (f32[128,128]{1,0:T(8,128)S(1)}, f32[128,128]{1,0:T(8,128)}, u32[]{:S(2)}) copy-start(f32[128,128]{1,0:T(8,128)} %copy-done.14) | copy-start | bytes 196612
  116.5 7.8 %copy-start.25 = (f32[2,128,128]{2,1,0:T(8,128)S(1)}, f32[2,128,128]{2,1,0:T(8,128)}, u32[]{:S(2)}) copy-start(f32[2,128,128]{2,1,0:T(8,128)} %copy-done.24) | copy-start | bytes 393220
  131.4 25.3 %all-to-all-start.1 = ((f32[32,1,128]{2,1,0:T(1,128)}), f32[32,1,128]{2,1,0:T(1,128)S(1)}, u32[]{:S(2)}, u32[]{:S(2)}) async-start(f32[32,1,128]{2,1,0:T(1,128)} %get-tuple-element.65), calls=%async_computation.1 | async-start | bytes 32768 | tf_op jit(solution)/shard_map/all_to_all | solution.py:555
  137.2 51.1 %collective-permute-start.6 = (bf16[2,8,32,128]{3,2,1,0:T(8,128)(2,1)}, bf16[2,8,32,128]{3,2,1,0:T(8,128)(2,1)S(1)}, u32[]{:S(2)}, u32[]{:S(2)}) collective-permute-start(bf16[2,8,32,128]{3,2,1,0:T(8,128)(2,1)} %get-tuple-element.68), channel_id=1, source_target_pairs={{0,1},{1,0},{2,3},{3,2},{4,5},{5,4},{6,7},{7,6},{8,9},{9,8},{10,11... | collective-permute-start | bytes 393224 | tf_op jit(solution)/shard_map/ppermute | solution.py:452
  138.9 49.5 %collective-permute-start.7 = (bf16[2,8,32,128]{3,2,1,0:T(8,128)(2,1)}, bf16[2,8,32,128]{3,2,1,0:T(8,128)(2,1)S(1)}, u32[]{:S(2)}, u32[]{:S(2)}) collective-permute-start(bf16[2,8,32,128]{3,2,1,0:T(8,128)(2,1)} %get-tuple-element.69), channel_id=1, source_target_pairs={{0,2},{1,3},{2,0},{3,1},{4,6},{5,7},{6,4},{7,5},{8,10},{9,11},{10,... | collective-permute-start | bytes 393224 | tf_op jit(solution)/shard_map/ppermute | solution.py:452
  156.7 4.4 %copy-start.27 = (f32[2,128,128]{2,1,0:T(8,128)S(1)}, f32[2,128,128]{2,1,0:T(8,128)}, u32[]{:S(2)}) copy-start(f32[2,128,128]{2,1,0:T(8,128)} %get-tuple-element.62.refs_1_.later_ref) | copy-start | bytes 393220
  156.7 4.4 %copy-start.28 = (f32[2,128,128]{2,1,0:T(8,128)S(1)}, f32[2,128,128]{2,1,0:T(8,128)}, u32[]{:S(2)}) copy-start(f32[2,128,128]{2,1,0:T(8,128)} %get-tuple-element.76.last_ref) | copy-start | bytes 393220
  163.4 27.0 %all-to-all-start.2 = ((f32[8,32,128]{2,1,0:T(8,128)}), f32[8,32,128]{2,1,0:T(8,128)S(1)}, u32[]{:S(2)}, u32[]{:S(2)}) async-start(f32[8,32,128]{2,1,0:T(8,128)} %bitcast.10), calls=%async_computation.2 | async-start | bytes 262144 | tf_op jit(solution)/shard_map/all_to_all | solution.py:458
  170.0 1.9 copy-start.6
  173.2 1.9 copy-start.33
  173.2 2.3 copy-start.8
  173.2 2.3 copy-start.11
  173.2 2.3 copy-start.13
  175.0 13.3 %collective-permute-start.8 = (bf16[2,8,32,128]{3,2,1,0:T(8,128)(2,1)S(1)}, bf16[2,8,32,128]{3,2,1,0:T(8,128)(2,1)S(1)}, u32[]{:S(2)}, u32[]{:S(2)}) collective-permute-start(bf16[2,8,32,128]{3,2,1,0:T(8,128)(2,1)S(1)} %copy-done.33), channel_id=1, source_target_pairs={{0,3},{1,2},{2,1},{3,0},{4,7},{5,6},{6,5},{7,4},{8,11},{9,10},{10,... | collective-permute-start | bytes 393224 | tf_op jit(solution)/shard_map/ppermute | solution.py:452
  177.6 10.8 %copy-start.9 = (bf16[256,4096]{1,0:T(8,128)(2,1)S(1)}, bf16[256,4096]{1,0:T(8,128)(2,1)}, u32[]{:S(2)}) copy-start(bf16[256,4096]{1,0:T(8,128)(2,1)} %get-tuple-element.67.col_ref.col_hbm) | copy-start | bytes 6291460
  181.2 7.1 %copy-start.3 = (bf16[2,128,32,128]{3,2,1,0:T(8,128)(2,1)S(1)}, bf16[2,128,32,128]{3,2,1,0:T(8,128)(2,1)}, u32[]{:S(2)}) copy-start(bf16[2,128,32,128]{3,2,1,0:T(8,128)(2,1)} %own_ref.6) | copy-start | bytes 6291460
  184.4 39.9 %collective-permute-start.15 = (bf16[2,40,32,128]{3,2,1,0:T(8,128)(2,1)}, bf16[2,40,32,128]{3,2,1,0:T(8,128)(2,1)}, u32[]{:S(2)}, u32[]{:S(2)}) collective-permute-start(bf16[2,40,32,128]{3,2,1,0:T(8,128)(2,1)} %get-tuple-element.87), channel_id=1, source_target_pairs={{0,1},{1,0},{2,3},{3,2},{4,5},{5,4},{6,7},{7,6},{8,9},{9,8},{10,11... | collective-permute-start | bytes 1966088 | tf_op jit(solution)/shard_map/ppermute | solution.py:452
  185.0 43.1 %collective-permute-start.16 = (bf16[2,24,32,128]{3,2,1,0:T(8,128)(2,1)}, bf16[2,24,32,128]{3,2,1,0:T(8,128)(2,1)}, u32[]{:S(2)}, u32[]{:S(2)}) collective-permute-start(bf16[2,24,32,128]{3,2,1,0:T(8,128)(2,1)} %get-tuple-element.88), channel_id=1, source_target_pairs={{0,2},{1,3},{2,0},{3,1},{4,6},{5,7},{6,4},{7,5},{8,10},{9,11},{10,... | collective-permute-start | bytes 1179656 | tf_op jit(solution)/shard_map/ppermute | solution.py:452
  190.4 20.3 %collective-permute-start.18 = (f32[32,128]{1,0:T(8,128)S(1)}, f32[32,128]{1,0:T(8,128)S(1)}, u32[]{:S(2)}, u32[]{:S(2)}) collective-permute-start(f32[32,128]{1,0:T(8,128)S(1)} %reduce_sum.19), channel_id=1, source_target_pairs={{0,1},{1,0},{2,3},{3,2},{4,5},{5,4},{6,7},{7,6},{8,9},{9,8},{10,11... | collective-permute-start | bytes 49160 | tf_op jit(solution)/shard_map/ppermute | solution.py:452
  190.5 23.8 %collective-permute-start.19 = (f32[32,128]{1,0:T(8,128)S(1)}, f32[32,128]{1,0:T(8,128)S(1)}, u32[]{:S(2)}, u32[]{:S(2)}) collective-permute-start(f32[32,128]{1,0:T(8,128)S(1)} %reduce_sum.19), channel_id=1, source_target_pairs={{0,2},{1,3},{2,0},{3,1},{4,6},{5,7},{6,4},{7,5},{8,10},{9,11},{10,... | collective-permute-start | bytes 49160 | tf_op jit(solution)/shard_map/ppermute | solution.py:452
  191.5 22.8 %collective-permute-start.20 = (f32[32,128]{1,0:T(8,128)S(1)}, f32[32,128]{1,0:T(8,128)S(1)}, u32[]{:S(2)}, u32[]{:S(2)}) collective-permute-start(f32[32,128]{1,0:T(8,128)S(1)} %reduce_sum.19), channel_id=1, source_target_pairs={{0,3},{1,2},{2,1},{3,0},{4,7},{5,6},{6,5},{7,4},{8,11},{9,10},{10,... | collective-permute-start | bytes 49160 | tf_op jit(solution)/shard_map/ppermute | solution.py:452
  199.2 11.6 %copy-start.19 = (bf16[2,24,32,128]{3,2,1,0:T(8,128)(2,1)S(1)}, bf16[2,24,32,128]{3,2,1,0:T(8,128)(2,1)}, u32[]{:S(2)}) copy-start(bf16[2,24,32,128]{3,2,1,0:T(8,128)(2,1)} %copy-done.18) | copy-start | bytes 1179652
  199.2 20.3 %copy-start.17 = (bf16[2,40,32,128]{3,2,1,0:T(8,128)(2,1)S(1)}, bf16[2,40,32,128]{3,2,1,0:T(8,128)(2,1)}, u32[]{:S(2)}) copy-start(bf16[2,40,32,128]{3,2,1,0:T(8,128)(2,1)} %copy-done.16) | copy-start | bytes 1966084
  199.2 20.3 %copy-start.23 = (bf16[2,24,32,128]{3,2,1,0:T(8,128)(2,1)S(1)}, bf16[2,24,32,128]{3,2,1,0:T(8,128)(2,1)}, u32[]{:S(2)}) copy-start(bf16[2,24,32,128]{3,2,1,0:T(8,128)(2,1)} %copy-done.22) | copy-start | bytes 1179652
  199.2 25.1 %copy-start.21 = (bf16[2,24,32,128]{3,2,1,0:T(8,128)(2,1)S(1)}, bf16[2,24,32,128]{3,2,1,0:T(8,128)(2,1)}, u32[]{:S(2)}) copy-start(bf16[2,24,32,128]{3,2,1,0:T(8,128)(2,1)} %copy-done.20) | copy-start | bytes 1179652
  210.7 19.1 %collective-permute-start.17 = (bf16[2,24,32,128]{3,2,1,0:T(8,128)(2,1)S(1)}, bf16[2,24,32,128]{3,2,1,0:T(8,128)(2,1)}, u32[]{:S(2)}, u32[]{:S(2)}) collective-permute-start(bf16[2,24,32,128]{3,2,1,0:T(8,128)(2,1)S(1)} %copy-done.19), channel_id=1, source_target_pairs={{0,3},{1,2},{2,1},{3,0},{4,7},{5,6},{6,5},{7,4},{8,11},{9,10},{10,... | collective-permute-start | bytes 1179656 | tf_op jit(solution)/shard_map/ppermute | solution.py:452
  215.0 9.3 %all-to-all-start.3 = ((f32[8,32,128]{2,1,0:T(8,128)}), f32[8,32,128]{2,1,0:T(8,128)S(1)}, u32[]{:S(2)}, u32[]{:S(2)}) async-start(f32[8,32,128]{2,1,0:T(8,128)} %broadcast_in_dim.8), calls=%async_computation.3 | async-start | bytes 262144 | tf_op jit(solution)/shard_map/all_to_all | solution.py:468
  219.5 25.8 %collective-permute-start.9 = (bf16[2,40,32,128]{3,2,1,0:T(8,128)(2,1)S(1)}, bf16[2,40,32,128]{3,2,1,0:T(8,128)(2,1)S(1)}, u32[]{:S(2)}, u32[]{:S(2)}) collective-permute-start(bf16[2,40,32,128]{3,2,1,0:T(8,128)(2,1)S(1)} %copy-done.17), channel_id=1, source_target_pairs={{0,1},{1,0},{2,3},{3,2},{4,5},{5,4},{6,7},{7,6},{8,9},{9,8},{10,11... | collective-permute-start | bytes 1966088 | tf_op jit(solution)/shard_map/ppermute | solution.py:452
  219.5 37.0 %collective-permute-start.10 = (bf16[2,24,32,128]{3,2,1,0:T(8,128)(2,1)S(1)}, bf16[2,24,32,128]{3,2,1,0:T(8,128)(2,1)S(1)}, u32[]{:S(2)}, u32[]{:S(2)}) collective-permute-start(bf16[2,24,32,128]{3,2,1,0:T(8,128)(2,1)S(1)} %copy-done.23), channel_id=1, source_target_pairs={{0,2},{1,3},{2,0},{3,1},{4,6},{5,7},{6,4},{7,5},{8,10},{9,11},{10,... | collective-permute-start | bytes 1179656 | tf_op jit(solution)/shard_map/ppermute | solution.py:452
  224.3 33.0 %collective-permute-start.11 = (bf16[2,24,32,128]{3,2,1,0:T(8,128)(2,1)S(1)}, bf16[2,24,32,128]{3,2,1,0:T(8,128)(2,1)S(1)}, u32[]{:S(2)}, u32[]{:S(2)}) collective-permute-start(bf16[2,24,32,128]{3,2,1,0:T(8,128)(2,1)S(1)} %copy-done.21), channel_id=1, source_target_pairs={{0,3},{1,2},{2,1},{3,0},{4,7},{5,6},{6,5},{7,4},{8,11},{9,10},{10,... | collective-permute-start | bytes 1179656 | tf_op jit(solution)/shard_map/ppermute | solution.py:452
  (11 other events, 10.8 us)
